TPU v7x, 256 devices: a whole 4x4x8 slice. The times are simulated.
256 devices in a mesh: dom: 64 (over x, z, core), rep: 4 (over y).
Axes of the slice: x: 4, y: 4, z: 8, core: 2. Of those that a mesh axis runs over, the one named last changes fastest.
Arguments:
- features: bfloat16 [524288, 128], P('dom'), may hold values from -6 to 6
- partition_map: int32 [524288], replicated, may hold values from 0 to 524287, as said below
- seed_ids: int32 [16384], P(('dom', 'rep')), may hold values from 0 to 524287, as said below
- hop1_ids: int32 [16384, 15], P(('dom', 'rep')), may hold values from 0 to 524287, as said below
- hop2_ids: int32 [16384, 15, 10], P(('dom', 'rep')), may hold values from 0 to 524287, as said below
- labels: int32 [16384], P(('dom', 'rep')), may hold values from 0 to 171
- self_one: bfloat16 [128, 256], replicated, may hold values from -0.5 to 0.5
- neigh_one: bfloat16 [128, 256], replicated, may hold values from -0.5 to 0.5
- bias_one: float32 [256], replicated, may hold values from -3 to 3
- self_two: bfloat16 [256, 172], replicated, may hold values from -0.375 to 0.375
- neigh_two: bfloat16 [256, 172], replicated, may hold values from -0.375 to 0.375
- bias_two: float32 [172], replicated, may hold values from -2 to 112, as said below
Outputs:
- seed_loss: float32 [16384], P(('dom', 'rep'))
- grad_self_one: float32 [128, 256], replicated
- grad_neigh_one: float32 [128, 256], replicated
- grad_bias_one: float32 [256], replicated
- grad_self_two: float32 [256, 172], replicated
- grad_neigh_two: float32 [256, 172], replicated
- grad_bias_two: float32 [172], replicated
Inputs may be any that keep to these rules, and one draw needn't show every extreme that they name: A permutation of 0 to 524287: node v is stored at position p = partition_map[v], in partition p // 8192, row p % 8192. Rows below 256 of each partition hold hub nodes. `seed_ids`: node ids. `hop1_ids`: node ids. `hop2_ids`: take one device's 64 seeds (an aligned block of seeds) with all their hop-1 and hop-2 ids, 10624 ids with repeats counted, and map them through partition_map: at most 607 positions fall in any one partition, and at most 83 fall in rows 256 and above of any one partition. Every device reaches both bounds. `bias_two`: class biases; in one draw all 172 lie within a window of width 4 (about -2 to 2, or about 108 to 112).
All inputs are finite; a program needn't handle non-finite values.
Results may differ from a plain program's by a relative error of at most 0.003.
Values may be sent and summed in bfloat16 or wider, within the bound.
A program may use at most 128 MiB of HBM per device.

v0:
```python
import functools

import jax
import jax.numpy as jnp
from jax import lax
from jax.experimental import pallas as pl
from jax.experimental.pallas import tpu as pltpu
from jax.sharding import PartitionSpec as P

HOT_DEV = 256
LANES = 128
MESH = pl.DeviceIdType.MESH
VMEM_LIMIT = 56 * 1024 * 1024


def round_up(value, unit):
    return -(-value // unit) * unit


def dot_tn(left, right):
    return lax.dot_general(left, right, (((0,), (0,)), ((), ())), preferred_element_type=jnp.float32)


def dot_nt(left, right):
    return lax.dot_general(left, right, (((1,), (1,)), ((), ())), preferred_element_type=jnp.float32)


def dot_nn(left, right):
    return jnp.dot(left, right, preferred_element_type=jnp.float32)


def plan_kernel(ids_ref, map_ref, req_ref, addr_ref, own_ref, slot_ref, val_ref, pos_ref, pieces_ref, *, parts, shift, stride, id_rows, cap_pad):
    rows = ids_ref.shape[0]
    blocks = rows // 8
    stored = map_ref[...]
    pieces = jnp.concatenate([stored >> 16, (stored >> 8) & 255, stored & 255], axis=1)
    pieces_ref[...] = pieces.astype(jnp.float32).T.astype(jnp.bfloat16)
    map_iota = lax.broadcasted_iota(jnp.int32, map_ref.shape, 0)
    lane_iota = lax.broadcasted_iota(jnp.int32, (LANES, 2 * LANES), 0)

    def lookup(step, carry):
        base = pl.multiple_of(step * 8, 8)
        tile = ids_ref[pl.ds(base, 8), :]
        high, low = tile >> 7, tile & (LANES - 1)
        for k in range(0, 8, 2):
            hot = [(map_iota == high[q : q + 1, :]).astype(jnp.bfloat16) for q in (k, k + 1)]
            found = dot_nn(pieces_ref[...], jnp.concatenate(hot, axis=1))
            found = found[:LANES] * 65536.0 + found[LANES : 2 * LANES] * 256.0 + found[2 * LANES :]
            lane = jnp.concatenate([low[k : k + 1, :], low[k + 1 : k + 2, :]], axis=1)
            picked = jnp.sum(jnp.where(lane_iota == lane, found, 0.0), axis=0, keepdims=True)
            pos_ref[pl.ds(base + k, 1), :] = picked[:, :LANES].astype(jnp.int32)
            pos_ref[pl.ds(base + k + 1, 1), :] = picked[:, LANES:].astype(jnp.int32)
        return carry

    lax.fori_loop(0, blocks, lookup, 0)
    position = pos_ref[...]
    owner = position >> shift
    local = position & ((1 << shift) - 1)
    row_iota = lax.broadcasted_iota(jnp.int32, (rows, LANES), 0)
    is_cold = (local >= HOT_DEV) & (row_iota < id_rows)
    owner_cold = jnp.where(is_cold, owner, -1)
    upper = (
        lax.broadcasted_iota(jnp.int32, (LANES, LANES), 0) <= lax.broadcasted_iota(jnp.int32, (LANES, LANES), 1)
    ).astype(jnp.bfloat16)
    ones = jnp.ones((LANES, LANES), jnp.bfloat16)
    below = (
        lax.broadcasted_iota(jnp.int32, (rows, rows), 1) < lax.broadcasted_iota(jnp.int32, (rows, rows), 0)
    ).astype(jnp.bfloat16)
    slot = jnp.full((rows, LANES), -1.0, jnp.float32)
    for part in range(parts):
        hit = owner_cold == part
        member = hit.astype(jnp.bfloat16)
        ahead = dot_nn(below, member).astype(jnp.bfloat16)
        running = dot_nn(member, upper) + dot_nn(ahead, ones)
        slot = jnp.where(hit, running - 1.0, slot)
    slot = slot.astype(jnp.int32)
    addr_ref[...] = owner * stride + jnp.where(is_cold, HOT_DEV + slot, local)
    own_ref[...] = owner_cold
    slot_ref[...] = slot
    val_ref[...] = local
    part_iota = lax.broadcasted_iota(jnp.int32, (parts, LANES), 0)
    slot_iota = lax.broadcasted_iota(jnp.int32, (cap_pad, LANES), 0)

    def place(step, table):
        base = pl.multiple_of(step * 8, 8)
        own8 = own_ref[pl.ds(base, 8), :]
        slot8 = slot_ref[pl.ds(base, 8), :]
        val8 = val_ref[pl.ds(base, 8), :]
        for k in range(0, 8, 2):
            lefts, rights = [], []
            for q in range(k, k + 2):
                val = val8[q : q + 1, :].astype(jnp.float32)
                top = jnp.floor(val * (1.0 / LANES))
                mine = part_iota == own8[q : q + 1, :]
                lefts.append(
                    jnp.concatenate(
                        [jnp.where(mine, top, 0.0), jnp.where(mine, val - top * LANES, 0.0)], axis=0
                    ).astype(jnp.bfloat16)
                )
                rights.append((slot_iota == slot8[q : q + 1, :]).astype(jnp.bfloat16))
            table = table + dot_nt(jnp.concatenate(lefts, axis=1), jnp.concatenate(rights, axis=1))
        return table

    table = lax.fori_loop(0, blocks, place, jnp.zeros((2 * parts, cap_pad), jnp.float32))
    request = (table[:parts] * LANES + table[parts:]).astype(jnp.int32)
    req_ref[...] = jnp.zeros(req_ref.shape, jnp.int32)
    for c in range(cap_pad // LANES):
        req_ref[:, c, :] = request[:, c * LANES : (c + 1) * LANES]


def plan(ids, partition_map, parts, node_rows, stride, id_rows, cap_pad):
    rows = ids.shape[0]
    kernel = functools.partial(
        plan_kernel,
        parts=parts,
        shift=node_rows.bit_length() - 1,
        stride=stride,
        id_rows=id_rows,
        cap_pad=cap_pad,
    )
    return pl.pallas_call(
        kernel,
        name="plan",
        out_shape=(
            jax.ShapeDtypeStruct((parts, round_up(cap_pad // LANES, 8), LANES), jnp.int32),
            jax.ShapeDtypeStruct((rows, LANES), jnp.int32),
        ),
        in_specs=[pl.BlockSpec(memory_space=pltpu.VMEM)] * 2,
        out_specs=(pl.BlockSpec(memory_space=pltpu.VMEM),) * 2,
        scratch_shapes=[pltpu.VMEM((rows, LANES), jnp.int32)] * 4
        + [pltpu.VMEM((3 * LANES, partition_map.size // LANES), jnp.bfloat16)],
        compiler_params=pltpu.CompilerParams(vmem_limit_bytes=VMEM_LIMIT),
        cost_estimate=pl.CostEstimate(flops=40_000_000, bytes_accessed=1_000_000, transcendentals=0),
    )(ids, partition_map.reshape(-1, LANES))


ROOT = 0.7978845608028654
CUBE = 0.044715


def gelu_pair(pre):
    square = pre * pre
    bend = jnp.tanh(ROOT * pre * (1.0 + CUBE * square))
    half = 0.5 * (1.0 + bend)
    slope = half + 0.5 * pre * (1.0 - bend * bend) * (ROOT * (1.0 + 3.0 * CUBE * square))
    return pre * half, slope


def tree_sum(values):
    while len(values) > 1:
        values = [a + b for a, b in zip(values[::2], values[1::2])] + (
            [values[-1]] if len(values) % 2 else []
        )
    return values[0]


def model_kernel(
    addr_ref, table_ref, label_ref, self_one, neigh_one, b_one_ref, self_two, neigh_two, b_two_ref,
    loss_ref, pack_ref,
    wide, x_buf, far_buf, own_buf, slope_buf, d_buf, *, seeds, fan_one, fan_two,
):
    feat = table_ref.shape[1]
    hidden = self_one.shape[1]
    hops = seeds * fan_one
    chunk = 64 if table_ref.shape[0] % 64 == 0 else 16

    def widen(step, carry):
        at = pl.ds(pl.multiple_of(step * chunk, chunk), chunk)
        wide[at, :] = table_ref[at, :].astype(jnp.float32)
        return carry

    lax.fori_loop(0, table_ref.shape[0] // chunk, widen, 0)

    def fetch(step, carry):
        j = step // (seeds // 8)
        block = step % (seeds // 8)
        base = pl.multiple_of(step * 8, 8)
        for k in range(8):
            hop = (block * 8 + k) * fan_one + j
            own_buf[pl.ds(base + k, 1), :] = wide[pl.ds(addr_ref[seeds + hop], 1), :]
            first = seeds + hops + hop * fan_two
            rows = [wide[pl.ds(addr_ref[first + m], 1), :] for m in range(fan_two)]
            far_buf[pl.ds(base + k, 1), :] = tree_sum(rows)
        return carry

    lax.fori_loop(0, hops // 8, fetch, 0)

    def fetch_seed(step, carry):
        base = pl.multiple_of(step * 8, 8)
        for k in range(8):
            own_buf[pl.ds(hops + base + k, 1), :] = wide[pl.ds(addr_ref[base + k], 1), :]
        return carry

    lax.fori_loop(0, seeds // 8, fetch_seed, 0)

    w_one = jnp.concatenate([self_one[...], neigh_one[...]], axis=0)
    w_two = jnp.concatenate([self_two[...], neigh_two[...]], axis=1)
    b_one = b_one_ref[...]
    row_sum = jnp.zeros((seeds, feat), jnp.float32)
    hid_sum = jnp.zeros((seeds, hidden), jnp.float32)
    for j in range(fan_one):
        at = slice(j * seeds, (j + 1) * seeds)
        own = own_buf[at, :]
        row_sum = row_sum + own
        x_buf[at, :feat] = own.astype(jnp.bfloat16)
        x_buf[at, feat:] = (far_buf[at, :] * (1.0 / fan_two)).astype(jnp.bfloat16)
    x_buf[hops:, :feat] = own_buf[hops:, :].astype(jnp.bfloat16)
    x_buf[hops:, feat:] = (row_sum * (1.0 / fan_one)).astype(jnp.bfloat16)
    act = None
    for j in range(fan_one + 1):
        at = slice(j * seeds, (j + 1) * seeds)
        act, slope = gelu_pair(dot_nn(x_buf[at, :], w_one) + b_one)
        act = act.astype(jnp.bfloat16)
        slope_buf[at, :] = slope
        if j < fan_one:
            hid_sum = hid_sum + act.astype(jnp.float32)
    hid = jnp.concatenate([act, (hid_sum * (1.0 / fan_one)).astype(jnp.bfloat16)], axis=1)
    logits = dot_nt(hid, w_two) + b_two_ref[...]
    shifted = logits - jnp.max(logits, axis=1, keepdims=True)
    log_probs = shifted - jnp.log(jnp.sum(jnp.exp(shifted), axis=1, keepdims=True))
    class_iota = lax.broadcasted_iota(jnp.int32, logits.shape, 1)
    diagonal = lax.broadcasted_iota(jnp.int32, (seeds, seeds), 0) == lax.broadcasted_iota(jnp.int32, (seeds, seeds), 1)
    label = jnp.sum(jnp.where(diagonal, label_ref[...].astype(jnp.float32), 0.0), axis=1, keepdims=True)
    target = (class_iota.astype(jnp.float32) == label).astype(jnp.float32)
    loss = jnp.sum(log_probs * target, axis=1, keepdims=True)
    loss_ref[...] = -jnp.sum(jnp.where(diagonal, loss, 0.0), axis=0, keepdims=True)
    d_logits = ((jnp.exp(log_probs) - target) * (1.0 / seeds)).astype(jnp.bfloat16)
    g_two = dot_tn(d_logits, hid)
    gb_two = jnp.sum(d_logits.astype(jnp.float32), axis=0, keepdims=True)
    d_hid = dot_nn(d_logits, w_two)
    d_hop = d_hid[:, hidden:] * (1.0 / fan_one)
    for j in range(fan_one + 1):
        at = slice(j * seeds, (j + 1) * seeds)
        d_pre = ((d_hop if j < fan_one else d_hid[:, :hidden]) * slope_buf[at, :]).astype(jnp.bfloat16)
        d_buf[at, :] = d_pre
    gb_one = dot_nn(jnp.ones((8, d_buf.shape[0]), jnp.bfloat16), d_buf[...])[:1]
    pack_gradients(pack_ref, dot_tn(x_buf[...], d_buf[...]), gb_one, g_two, gb_two)


def model(addr, table, labels, self_one, neigh_one, bias_one, self_two, neigh_two, bias_two, fan_one, fan_two, pack_rows):
    seeds = labels.shape[0]
    feat, hidden = self_one.shape
    classes = self_two.shape[1]
    total = seeds * (1 + fan_one)
    vmem = pl.BlockSpec(memory_space=pltpu.VMEM)
    return pl.pallas_call(
        functools.partial(model_kernel, seeds=seeds, fan_one=fan_one, fan_two=fan_two),
        name="model",
        out_shape=(
            jax.ShapeDtypeStruct((1, seeds), jnp.float32),
            jax.ShapeDtypeStruct((pack_rows, LANES), jnp.float32),
        ),
        in_specs=[pl.BlockSpec(memory_space=pltpu.SMEM)] + [vmem] * 8,
        out_specs=(vmem,) * 2,
        scratch_shapes=[
            pltpu.VMEM(table.shape, jnp.float32),
            pltpu.VMEM((total, 2 * feat), jnp.bfloat16),
            pltpu.VMEM((total - seeds, feat), jnp.float32),
            pltpu.VMEM((total, feat), jnp.float32),
            pltpu.VMEM((total, hidden), jnp.float32),
            pltpu.VMEM((total, hidden), jnp.bfloat16),
        ],
        compiler_params=pltpu.CompilerParams(vmem_limit_bytes=VMEM_LIMIT),
        cost_estimate=pl.CostEstimate(flops=100_000_000, bytes_accessed=4_000_000, transcendentals=0),
    )(
        addr,
        table,
        labels.reshape(1, seeds),
        self_one,
        neigh_one,
        bias_one.reshape(1, hidden),
        self_two.T,
        neigh_two.T,
        bias_two.reshape(1, classes),
    )


def exchange_kernel(
    req_ref, feat_ref, out_ref, inbox, wanted, wide, stage, send,
    local_sem, req_send, req_recv, hub_send, hub_recv, row_send, row_recv, *, parts, asks,
):
    node_rows = feat_ref.shape[0]
    cap_row = send.shape[1]
    me = lax.axis_index("dom")
    bits = parts.bit_length() - 1
    barrier = pltpu.get_barrier_semaphore()

    def partner(mask):
        other = me ^ mask
        return other, {"dom": other}

    def greet(step, carry):
        pl.semaphore_signal(barrier, inc=1, device_id=partner(step)[1], device_id_type=MESH)
        return carry

    lax.fori_loop(1, parts, greet, 0)
    hub_at = pl.ds(0, HOT_DEV)
    ask_at = pl.ds(0, asks)
    keep_req = pltpu.make_async_copy(req_ref.at[me], inbox.at[me], local_sem.at[0])
    keep_req.start()
    keep_hub = pltpu.make_async_copy(feat_ref.at[hub_at], out_ref.at[me, hub_at], local_sem.at[1])
    keep_hub.start()
    pl.semaphore_wait(barrier, parts - 1)

    def ask(step, carry):
        other, at = partner(parts - step)
        pltpu.make_async_remote_copy(
            req_ref.at[other, ask_at], inbox.at[me, ask_at], req_send, req_recv, device_id=at, device_id_type=MESH
        ).start()
        return carry

    lax.fori_loop(1, parts, ask, 0)
    keep_hub.wait()

    def held(level, index):
        return me ^ (index * (parts >> level))

    def share(level):
        at = partner(parts >> (level + 1))[1]

        def one(index, carry):
            slot = held(level, index)
            pltpu.make_async_remote_copy(
                out_ref.at[slot, hub_at], out_ref.at[slot, hub_at], hub_send.at[level], hub_recv.at[level],
                device_id=at, device_id_type=MESH,
            ).start()
            return carry

        lax.fori_loop(0, 1 << level, one, 0)

    def shared(level):
        some = out_ref.at[pl.ds(0, 1 << level), hub_at]
        return pltpu.make_async_remote_copy(
            some, some, hub_send.at[level], hub_recv.at[level], device_id=partner(1)[1], device_id_type=MESH
        )

    share(0)

    def widen(step, carry):
        at = pl.ds(pl.multiple_of(step * 64, 64), 64)
        wide[at, :] = feat_ref[at, :].astype(jnp.float32)
        return carry

    lax.fori_loop(0, node_rows // 64, widen, 0)
    most = pl.ds(0, parts - 1)
    asked = pltpu.make_async_remote_copy(
        req_ref.at[most, ask_at], inbox.at[most, ask_at], req_send, req_recv,
        device_id=partner(1)[1], device_id_type=MESH,
    )
    keep_req.wait()
    asked.wait_recv()
    to_scalar = pltpu.make_async_copy(inbox.at[:, ask_at], wanted, local_sem.at[2])
    to_scalar.start()
    to_scalar.wait()

    def collect(other):
        def block(step, carry):
            base = pl.multiple_of(step * 16, 16)
            row = step // (LANES // 16)
            lane = lax.rem(step, LANES // 16) * 16
            for k in range(16):
                stage[pl.ds(base + k, 1), :] = wide[pl.ds(wanted[other, row, lane + k], 1), :]
            return carry

        lax.fori_loop(0, cap_row // 16, block, 0)
        return stage[...].astype(jnp.bfloat16)

    rows_at = pl.ds(HOT_DEV, cap_row)

    def serve(step, carry):
        other, at = partner(parts - step)
        send[other] = collect(other)
        pltpu.make_async_remote_copy(
            send.at[other], out_ref.at[me, rows_at], row_send, row_recv, device_id=at, device_id_type=MESH
        ).start()
        return carry

    served = 1
    for level in range(1, bits):
        until = max(1, parts * (level - 1) // bits)
        lax.fori_loop(served, until, serve, 0)
        served = until
        shared(level - 1).wait_recv()
        share(level)
    lax.fori_loop(served, parts, serve, 0)
    out_ref[me, HOT_DEV:, :] = collect(me)
    rows = pltpu.make_async_remote_copy(
        send.at[most], out_ref.at[most, rows_at], row_send, row_recv, device_id=partner(1)[1], device_id_type=MESH
    )
    asked.wait_send()
    shared(bits - 1).wait_recv()
    for level in range(bits):
        shared(level).wait_send()
    rows.wait()


def exchange(request, features, cap_row, asks):
    parts = lax.axis_size("dom")
    bits = parts.bit_length() - 1
    node_rows, feat = features.shape
    vmem = pl.BlockSpec(memory_space=pltpu.VMEM)
    return pl.pallas_call(
        functools.partial(exchange_kernel, parts=parts, asks=asks),
        name="exchange",
        out_shape=jax.ShapeDtypeStruct((parts, HOT_DEV + cap_row, feat), features.dtype),
        in_specs=[vmem, vmem],
        out_specs=vmem,
        scratch_shapes=[
            pltpu.VMEM(request.shape, jnp.int32),
            pltpu.SMEM((parts, asks, LANES), jnp.int32),
            pltpu.VMEM((node_rows, feat), jnp.float32),
            pltpu.VMEM((cap_row, feat), jnp.float32),
            pltpu.VMEM((parts, cap_row, feat), features.dtype),
            pltpu.SemaphoreType.DMA((3,)),
            pltpu.SemaphoreType.DMA,
            pltpu.SemaphoreType.DMA,
            pltpu.SemaphoreType.DMA((bits,)),
            pltpu.SemaphoreType.DMA((bits,)),
            pltpu.SemaphoreType.DMA,
            pltpu.SemaphoreType.DMA,
        ],
        compiler_params=pltpu.CompilerParams(collective_id=2, has_side_effects=True, vmem_limit_bytes=VMEM_LIMIT),
    )(request, features)


def pack_plan(feat, hidden, classes):
    halves = hidden // LANES
    one = 2 * feat * halves
    high = round_up(classes, 8)
    tail = one + 2 * halves * high
    return halves, one, high, tail, tail + 8


def pack_gradients(pack_ref, g_one, gb_one, g_two, gb_two):
    hidden, feat = g_one.shape[1], g_one.shape[0] // 2
    classes = g_two.shape[0]
    halves, one, high, tail, used = pack_plan(feat, hidden, classes)
    for h in range(halves):
        pack_ref[h * 2 * feat : (h + 1) * 2 * feat, :] = g_one[:, h * LANES : (h + 1) * LANES]
    pack_ref[one:, :] = jnp.zeros((pack_ref.shape[0] - one, LANES), jnp.float32)
    for h in range(2 * halves):
        pack_ref[one + h * high : one + h * high + classes, :] = g_two[:, h * LANES : (h + 1) * LANES]
    for h in range(halves):
        pack_ref[tail + h : tail + h + 1, :] = gb_one[:, h * LANES : (h + 1) * LANES]
    pack_ref[tail + halves : tail + halves + 1, :] = gb_two[:, :LANES]
    pack_ref[tail + halves + 1 : tail + halves + 2, : classes - LANES] = gb_two[:, LANES:]


def unpack_kernel(pack_ref, self_one, neigh_one, bias_one, self_two, neigh_two, bias_two):
    feat, hidden = self_one.shape
    classes = self_two.shape[0]
    halves, one, high, tail, used = pack_plan(feat, hidden, classes)
    for h in range(halves):
        cols = slice(h * LANES, (h + 1) * LANES)
        at = h * 2 * feat
        self_one[:, cols] = pack_ref[at : at + feat, :]
        neigh_one[:, cols] = pack_ref[at + feat : at + 2 * feat, :]
        at = one + h * high
        self_two[:, cols] = pack_ref[at : at + classes, :]
        at = one + (halves + h) * high
        neigh_two[:, cols] = pack_ref[at : at + classes, :]
        bias_one[:, cols] = pack_ref[tail + h : tail + h + 1, :]
    bias_two[:, :LANES] = pack_ref[tail + halves : tail + halves + 1, :]
    bias_two[:, LANES:] = pack_ref[tail + halves + 1 : tail + halves + 2, : classes - LANES]


def unpack(packed, feat, hidden, classes):
    vmem = pl.BlockSpec(memory_space=pltpu.VMEM)
    shapes = [(feat, hidden), (feat, hidden), (1, hidden), (classes, hidden), (classes, hidden), (1, classes)]
    return pl.pallas_call(
        unpack_kernel,
        name="unpack",
        out_shape=tuple(jax.ShapeDtypeStruct(shape, jnp.float32) for shape in shapes),
        in_specs=[vmem],
        out_specs=(vmem,) * 6,
        compiler_params=pltpu.CompilerParams(vmem_limit_bytes=VMEM_LIMIT),
    )(packed)


def reduce_kernel(
    part_ref, out_ref, near_box, middle, far_box, gathered, send_sem, recv_sem, *, n_dom, n_rep, near,
):
    count = n_dom * n_rep
    far = count // near
    rows = part_ref.shape[0] // count
    span = far * rows
    me = lax.axis_index("dom") * n_rep + lax.axis_index("rep")
    here, there = lax.rem(me, near), me // near
    barrier = pltpu.get_barrier_semaphore()

    def place(index):
        return {"dom": index // n_rep, "rep": lax.rem(index, n_rep)}

    def near_peer(step):
        other = lax.rem(here + step, near)
        return other, place(there * near + other)

    def far_peer(step):
        other = lax.rem(there + step, far)
        return other, place(other * near + here)

    def wide_at(index):
        return pl.ds(pl.multiple_of(index * span, 8), span)

    def thin_at(index):
        return pl.ds(pl.multiple_of(index * rows, 8), rows)

    def greet_near(step, carry):
        pl.semaphore_signal(barrier, inc=1, device_id=near_peer(step)[1], device_id_type=MESH)
        return carry

    def greet_far(step, carry):
        pl.semaphore_signal(barrier, inc=1, device_id=far_peer(step)[1], device_id_type=MESH)
        return carry

    lax.fori_loop(1, near, greet_near, 0)
    lax.fori_loop(1, far, greet_far, 0)
    pl.semaphore_wait(barrier, near + far - 2)

    def copy(source, target, stage, where):
        return pltpu.make_async_remote_copy(
            source, target, send_sem.at[stage], recv_sem.at[stage], device_id=where, device_id_type=MESH
        )

    def out_near(step, carry):
        other, where = near_peer(step)
        copy(part_ref.at[wide_at(other)], near_box.at[wide_at(here)], 0, where).start()
        return carry

    lax.fori_loop(1, near, out_near, 0)
    some = pl.ds(0, (near - 1) * span)
    first = copy(part_ref.at[some], near_box.at[some], 0, near_peer(1)[1])
    first.wait_recv()

    def add_near(step, total):
        return total + near_box[wide_at(near_peer(step)[0]), :]

    middle[...] = lax.fori_loop(1, near, add_near, part_ref[wide_at(here), :])

    def out_far(step, carry):
        other, where = far_peer(step)
        copy(middle.at[thin_at(other)], far_box.at[thin_at(there)], 1, where).start()
        return carry

    lax.fori_loop(1, far, out_far, 0)
    some = pl.ds(0, (far - 1) * rows)
    second = copy(middle.at[some], far_box.at[some], 1, far_peer(1)[1])
    second.wait_recv()

    def add_far(step, total):
        return total + far_box[thin_at(far_peer(step)[0]), :]

    total = lax.fori_loop(1, far, add_far, middle[thin_at(there), :])
    mine = here * far + there
    gathered[mine] = total.astype(gathered.dtype)

    def back_far(step, carry):
        copy(gathered.at[mine], gathered.at[mine], 2, far_peer(step)[1]).start()
        return carry

    lax.fori_loop(1, far, back_far, 0)
    some = gathered.at[pl.ds(0, far - 1)]
    third = copy(some, some, 2, far_peer(1)[1])
    third.wait_recv()
    group = gathered.at[pl.ds(here * far, far)]

    def back_near(step, carry):
        copy(group, group, 3, near_peer(step)[1]).start()
        return carry

    lax.fori_loop(1, near, back_near, 0)
    some = gathered.at[pl.ds(0, (near - 1) * far)]
    fourth = copy(some, some, 3, near_peer(1)[1])
    fourth.wait_recv()
    first.wait_send()
    second.wait_send()
    third.wait_send()
    fourth.wait_send()
    for index in range(count):
        out_ref[index * rows : (index + 1) * rows, :] = gathered[index].astype(jnp.float32)


def sum_everywhere(pieces):
    n_dom, n_rep = lax.axis_size("dom"), lax.axis_size("rep")
    count = n_dom * n_rep
    near = 8
    far = count // near
    rows = pieces.shape[0] // count
    vmem = pl.BlockSpec(memory_space=pltpu.VMEM)
    return pl.pallas_call(
        functools.partial(reduce_kernel, n_dom=n_dom, n_rep=n_rep, near=near),
        name="sum_everywhere",
        out_shape=jax.ShapeDtypeStruct(pieces.shape, jnp.float32),
        in_specs=[vmem],
        out_specs=vmem,
        scratch_shapes=[
            pltpu.VMEM(pieces.shape, jnp.float32),
            pltpu.VMEM((far * rows, LANES), jnp.float32),
            pltpu.VMEM((far * rows, LANES), jnp.float32),
            pltpu.VMEM((count, rows, LANES), jnp.bfloat16),
            pltpu.SemaphoreType.DMA((4,)),
            pltpu.SemaphoreType.DMA((4,)),
        ],
        compiler_params=pltpu.CompilerParams(collective_id=1, has_side_effects=True, vmem_limit_bytes=VMEM_LIMIT),
    )(pieces)


def shards(
    features, partition_map, seed_ids, hop1_ids, hop2_ids, labels,
    self_one, neigh_one, bias_one, self_two, neigh_two, bias_two,
):
    parts = lax.axis_size("dom")
    count = parts * lax.axis_size("rep")
    seeds = seed_ids.shape[0]
    fan_one = hop1_ids.shape[1]
    fan_two = hop2_ids.shape[2]
    node_rows, feat = features.shape
    tree_rows = 1 + fan_one + fan_one * fan_two
    cold_cap = tree_rows // 2 * (seeds // parts)
    cap_row = round_up(cold_cap, 16)
    cap_pad = round_up(cold_cap, LANES)
    stride = HOT_DEV + cap_row
    total = seeds * tree_rows
    id_rows = total // LANES
    spare = round_up(id_rows, 8) * LANES - total
    wanted = [seed_ids, hop1_ids.reshape(-1), hop2_ids.reshape(-1), jnp.zeros((spare,), jnp.int32)]
    ids = jnp.concatenate(wanted).reshape(-1, LANES)
    request, addr = plan(ids, partition_map, parts, node_rows, stride, id_rows, cap_pad)
    table = exchange(request, features, cap_row, cap_pad // LANES).reshape(parts * stride, feat)
    hidden, classes = self_two.shape
    used = pack_plan(feat, hidden, classes)[-1]
    pack_rows = count * round_up(-(-used // count), 8)
    loss, pieces = model(
        addr.reshape(-1), table, labels, self_one, neigh_one, bias_one, self_two, neigh_two, bias_two,
        fan_one, fan_two, pack_rows,
    )
    grads = unpack(sum_everywhere(pieces), feat, hidden, classes)
    return (
        loss.reshape(-1), grads[0], grads[1], grads[2].reshape(-1),
        grads[3].T, grads[4].T, grads[5].reshape(-1),
    )


def solution(mesh):
    return jax.shard_map(
        shards,
        mesh=mesh,
        in_specs=(
            P("dom", None),
            P(),
            P(("dom", "rep")),
            P(("dom", "rep"), None),
            P(("dom", "rep"), None, None),
            P(("dom", "rep")),
            P(),
            P(),
            P(),
            P(),
            P(),
            P(),
        ),
        out_specs=(P(("dom", "rep")), P(), P(), P(), P(), P(), P()),
        check_vma=False,
    )
```

profile of v0, /device:TPU:1, one launch (start us, length us, event | category | flops | bytes accessed | tf_op | source)
XLA Modules:
  0.0 232.3 jit_solution(6523113831840084648)
XLA Ops:
  0.6 0.8 copy.19
  1.4 0.1 reshape.50
  1.6 1.2 copy.20
  2.8 0.3 reshape.51
  3.1 1.3 concatenate.3
  4.4 50.9 %plan.1 = (s32[64,8,128]{2,1,0:T(8,128)}, s32[88,128]{1,0:T(8,128)}) custom-call(s32[88,128]{1,0:T(8,128)} %bitcast.16, s32[4096,128]{1,0:T(8,128)} %bitcast.15), custom_call_target="tpu_custom_call" | custom-call | flops 40000000 | bytes 1000000 | tf_op jit(solution)/shard_map/plan/pallas_call | solution.py:121
  55.3 115.8 %exchange.1 = bf16[64,352,128]{2,1,0:T(8,128)(2,1)} custom-call(s32[64,8,128]{2,1,0:T(8,128)} %get-tuple-element.18.req_ref, bf16[8192,128]{1,0:T(8,128)(2,1)} %feat_ref.1), custom_call_target="tpu_custom_call" | custom-call | tf_op jit(solution)/shard_map/exchange/pallas_call | solution.py:402
  171.1 18.7 %model.1 = (f32[1,64]{1,0:T(1,128)}, f32[2048,128]{1,0:T(8,128)}) custom-call(s32[11264]{0:T(1024)} %bitcast.19, bf16[22528,128]{1,0:T(8,128)(2,1)} %bitcast.14, s32[1,64]{1,0:T(1,128)} %bitcast.22, bf16[128,256]{1,0:T(8,128)(2,1)} %self_one.1, bf16[128,256]{1,0:T(8,128)(2,1)} %neigh_one.1, f32[1,256]{1,0:T(1,128)} %bitcast.20, bf16[172,256]{1,0:T(8,128)(2,1)} %bitcast.17, ...), custom_call_target="tpu_custom_call" | custom-call | flops 100000000 | bytes 4000000 | tf_op jit(solution)/shard_map/model/pallas_call | solution.py:246
  189.8 40.4 %sum_everywhere.1.pack_ref = f32[2048,128]{1,0:T(8,128)} custom-call(f32[2048,128]{1,0:T(8,128)} %get-tuple-element.20.part_ref), custom_call_target="tpu_custom_call" | custom-call | tf_op jit(solution)/shard_map/sum_everywhere/pallas_call | solution.py:590
  230.3 2.1 unpack.1
  (1 shorter events, 0.0 us)
where the time goes:
time: 233 us; the launch traced here: 232 us
  Pallas kernels  228 us (98%)
  local copies, waits for them, and re-layouts  3.74 us (2%)
    pallas_call x1, Pallas kernels, exchange(): pl.pallas_call(functools.partial(exchange_kernel, parts=parts, asks=asks)...  116 us
    pallas_call x1, Pallas kernels, plan(): pl.pallas_call(kernel, name='plan', out_shape=(jax.ShapeDtypeStruct((part...  50.9 us
    pallas_call x1, Pallas kernels, sum_everywhere(): pl.pallas_call(functools.partial(reduce_kernel, n_dom=n_dom, n_rep=n_rep,...  40.4 us
    pallas_call x1, Pallas kernels, model(): pl.pallas_call(functools.partial(model_kernel, seeds=seeds, fan_one=fan_o...  18.7 us

commit v1 on v0

--- a/solution.py
+++ b/solution.py
@@ -29,109 +29,291 @@
     return jnp.dot(left, right, preferred_element_type=jnp.float32)
 
 
-def plan_kernel(ids_ref, map_ref, req_ref, addr_ref, own_ref, slot_ref, val_ref, pos_ref, pieces_ref, *, parts, shift, stride, id_rows, cap_pad):
-    rows = ids_ref.shape[0]
-    blocks = rows // 8
-    stored = map_ref[...]
-    pieces = jnp.concatenate([stored >> 16, (stored >> 8) & 255, stored & 255], axis=1)
-    pieces_ref[...] = pieces.astype(jnp.float32).T.astype(jnp.bfloat16)
-    map_iota = lax.broadcasted_iota(jnp.int32, map_ref.shape, 0)
-    lane_iota = lax.broadcasted_iota(jnp.int32, (LANES, 2 * LANES), 0)
-
-    def lookup(step, carry):
-        base = pl.multiple_of(step * 8, 8)
-        tile = ids_ref[pl.ds(base, 8), :]
-        high, low = tile >> 7, tile & (LANES - 1)
-        for k in range(0, 8, 2):
-            hot = [(map_iota == high[q : q + 1, :]).astype(jnp.bfloat16) for q in (k, k + 1)]
-            found = dot_nn(pieces_ref[...], jnp.concatenate(hot, axis=1))
-            found = found[:LANES] * 65536.0 + found[LANES : 2 * LANES] * 256.0 + found[2 * LANES :]
-            lane = jnp.concatenate([low[k : k + 1, :], low[k + 1 : k + 2, :]], axis=1)
-            picked = jnp.sum(jnp.where(lane_iota == lane, found, 0.0), axis=0, keepdims=True)
-            pos_ref[pl.ds(base + k, 1), :] = picked[:, :LANES].astype(jnp.int32)
-            pos_ref[pl.ds(base + k + 1, 1), :] = picked[:, LANES:].astype(jnp.int32)
-        return carry
-
-    lax.fori_loop(0, blocks, lookup, 0)
+N_X, N_Z = 4, 8
+ID_ROWS = 83
+HUB_ROWS = 64 * HOT_DEV
+
+
+def place_ids(hop2_ref, hop1_ref, seed_ref, ids_ref):
+    fan_two, fan_one, seeds = hop2_ref.shape
+    half = fan_two // 2
+    ids_ref[...] = jnp.zeros(ids_ref.shape, jnp.int32)
+    for m in range(half):
+        at = slice(m * fan_one, (m + 1) * fan_one)
+        ids_ref[at, :seeds] = hop2_ref[m]
+        ids_ref[at, seeds:] = hop2_ref[half + m]
+    top = half * fan_one
+    ids_ref[top : top + 8, :seeds] = hop1_ref[:8, :]
+    ids_ref[top : top + fan_one - 8, seeds:] = hop1_ref[8:, :]
+    ids_ref[top + fan_one - 8 : top + fan_one - 7, seeds:] = seed_ref[...]
+
+
+def gather_map(first, smem_ref, map_ref, stage):
+    for r in range(stage.shape[0] // LANES):
+        for i in range(LANES):
+            stage[pl.ds(r * LANES + i, 1), :] = map_ref[pl.ds(smem_ref[first + r, i] >> 7, 1), :]
+
+
+def pick_lanes(first, ids_ref, stage, pos_ref):
+    sub_iota = lax.broadcasted_iota(jnp.int32, (LANES, LANES), 0)
+    lane_iota = lax.broadcasted_iota(jnp.int32, (LANES, LANES), 1)
+    for r in range(stage.shape[0] // LANES):
+        got = stage[r * LANES : (r + 1) * LANES, :]
+        pieces = jnp.concatenate([got >> 16, (got >> 8) & 255, got & 255], axis=0)
+        pieces = pieces.astype(jnp.float32).astype(jnp.bfloat16)
+        low = ids_ref[pl.ds(first + r, 1), :] & (LANES - 1)
+        hot = (sub_iota == low).astype(jnp.float32).astype(jnp.bfloat16)
+        found = dot_nn(pieces, hot)
+        found = found[:LANES] * 65536.0 + found[LANES : 2 * LANES] * 256.0 + found[2 * LANES :]
+        picked = jnp.sum(jnp.where(sub_iota == lane_iota, found, 0.0), axis=0, keepdims=True)
+        pos_ref[pl.ds(first + r, 1), :] = picked.astype(jnp.int32)
+
+
+def lookup_step(step, ids_ref, smem_ref, map_ref, stage_a, stage_b, pos_ref):
+    first = step * 4
+    gather_map(first, smem_ref, map_ref, stage_a)
+
+    pick_lanes(first, ids_ref, stage_a, pos_ref)
+    gather_map(first + 2, smem_ref, map_ref, stage_b)
+    pick_lanes(first + 2, ids_ref, stage_b, pos_ref)
+
+
+def assign(pos_ref, own_ref, val_ref, slot_ref, addr_ref, req_ref, *, parts, shift, cap_row):
+    rows = pos_ref.shape[0]
     position = pos_ref[...]
     owner = position >> shift
     local = position & ((1 << shift) - 1)
     row_iota = lax.broadcasted_iota(jnp.int32, (rows, LANES), 0)
-    is_cold = (local >= HOT_DEV) & (row_iota < id_rows)
-    owner_cold = jnp.where(is_cold, owner, -1)
-    upper = (
-        lax.broadcasted_iota(jnp.int32, (LANES, LANES), 0) <= lax.broadcasted_iota(jnp.int32, (LANES, LANES), 1)
-    ).astype(jnp.bfloat16)
-    ones = jnp.ones((LANES, LANES), jnp.bfloat16)
-    below = (
-        lax.broadcasted_iota(jnp.int32, (rows, rows), 1) < lax.broadcasted_iota(jnp.int32, (rows, rows), 0)
-    ).astype(jnp.bfloat16)
-    slot = jnp.full((rows, LANES), -1.0, jnp.float32)
-    for part in range(parts):
-        hit = owner_cold == part
-        member = hit.astype(jnp.bfloat16)
-        ahead = dot_nn(below, member).astype(jnp.bfloat16)
-        running = dot_nn(member, upper) + dot_nn(ahead, ones)
-        slot = jnp.where(hit, running - 1.0, slot)
-    slot = slot.astype(jnp.int32)
-    addr_ref[...] = owner * stride + jnp.where(is_cold, HOT_DEV + slot, local)
-    own_ref[...] = owner_cold
-    slot_ref[...] = slot
+    is_cold = (local >= HOT_DEV) & (row_iota < ID_ROWS)
+    own_ref[...] = jnp.where(is_cold, owner, -1)
     val_ref[...] = local
     part_iota = lax.broadcasted_iota(jnp.int32, (parts, LANES), 0)
-    slot_iota = lax.broadcasted_iota(jnp.int32, (cap_pad, LANES), 0)
-
-    def place(step, table):
-        base = pl.multiple_of(step * 8, 8)
-        own8 = own_ref[pl.ds(base, 8), :]
-        slot8 = slot_ref[pl.ds(base, 8), :]
-        val8 = val_ref[pl.ds(base, 8), :]
-        for k in range(0, 8, 2):
-            lefts, rights = [], []
-            for q in range(k, k + 2):
-                val = val8[q : q + 1, :].astype(jnp.float32)
-                top = jnp.floor(val * (1.0 / LANES))
-                mine = part_iota == own8[q : q + 1, :]
-                lefts.append(
-                    jnp.concatenate(
-                        [jnp.where(mine, top, 0.0), jnp.where(mine, val - top * LANES, 0.0)], axis=0
-                    ).astype(jnp.bfloat16)
-                )
-                rights.append((slot_iota == slot8[q : q + 1, :]).astype(jnp.bfloat16))
-            table = table + dot_nt(jnp.concatenate(lefts, axis=1), jnp.concatenate(rights, axis=1))
-        return table
-
-    table = lax.fori_loop(0, blocks, place, jnp.zeros((2 * parts, cap_pad), jnp.float32))
-    request = (table[:parts] * LANES + table[parts:]).astype(jnp.int32)
-    req_ref[...] = jnp.zeros(req_ref.shape, jnp.int32)
-    for c in range(cap_pad // LANES):
-        req_ref[:, c, :] = request[:, c * LANES : (c + 1) * LANES]
-
-
-def plan(ids, partition_map, parts, node_rows, stride, id_rows, cap_pad):
-    rows = ids.shape[0]
-    kernel = functools.partial(
-        plan_kernel,
-        parts=parts,
-        shift=node_rows.bit_length() - 1,
-        stride=stride,
-        id_rows=id_rows,
-        cap_pad=cap_pad,
+    slot_iota = lax.broadcasted_iota(jnp.int32, (LANES, LANES), 0)
+    upper = lax.broadcasted_iota(jnp.int32, (LANES, 2 * LANES), 0) <= lax.broadcasted_iota(
+        jnp.int32, (LANES, 2 * LANES), 1
     )
+    upper = upper.astype(jnp.float32).astype(jnp.bfloat16)
+
+    def block(step, carry):
+        base, table = carry
+        at = pl.ds(pl.multiple_of(step * 8, 8), 8)
+        own8 = own_ref[at, :]
+        val8 = val_ref[at, :].astype(jnp.float32)
+        top8 = jnp.floor(val8 * (1.0 / LANES))
+        low8 = val8 - top8 * LANES
+        slots, lefts = [], []
+        for q in range(8):
+            mine = part_iota == own8[q : q + 1, :]
+            counts = dot_nn(mine.astype(jnp.float32).astype(jnp.bfloat16), upper)
+            slots.append(jnp.sum(jnp.where(mine, counts[:, :LANES] + base, 0.0), axis=0, keepdims=True) - 1.0)
+            base = base + counts[:, LANES:]
+            lefts.append(
+                jnp.concatenate(
+                    [jnp.where(mine, top8[q : q + 1, :], 0.0), jnp.where(mine, low8[q : q + 1, :], 0.0)], axis=0
+                ).astype(jnp.bfloat16)
+            )
+        slot8 = jnp.concatenate(slots, axis=0).astype(jnp.int32)
+        slot_ref[at, :] = slot8
+        for q in range(0, 8, 2):
+            rights = [
+                (slot_iota == slot8[k : k + 1, :]).astype(jnp.float32).astype(jnp.bfloat16) for k in (q, q + 1)
+            ]
+            table = table + dot_nt(
+                jnp.concatenate([lefts[q], lefts[q + 1]], axis=1), jnp.concatenate(rights, axis=1)
+            )
+        return base, table
+
+    start = (jnp.zeros((parts, LANES), jnp.float32), jnp.zeros((2 * parts, LANES), jnp.float32))
+    table = lax.fori_loop(0, rows // 8, block, start)[1]
+    request = (table[:parts] * LANES + table[parts:]).astype(jnp.int32) & ((1 << shift) - 1)
+    for p in range(parts):
+        req_ref[p, 0:1, :] = request[p : p + 1, :]
+    hot_addr = (owner & 1) * (HUB_ROWS // 2) + (owner >> 1) * HOT_DEV + (local & (HOT_DEV - 1))
+    addr_ref[...] = jnp.where(is_cold, HUB_ROWS + owner * cap_row + slot_ref[...], hot_addr)
+
+
+def front_kernel(
+    hop2_ref, hop1_ref, seed_ref, map_hbm, feat_hbm,
+    table_ref, addr_ref,
+    ids_ref, pos_ref, own_ref, val_ref, slot_ref, map_ref, feat_ref, wide, stage_a, stage_b, row_stage,
+    req_ref, inbox, send, ids_smem, wanted,
+    local_sem, req_send, req_recv, hub_send, hub_recv, row_send, row_recv, *, parts, shift, cap_row,
+):
+    node_rows = feat_ref.shape[0]
+    me = lax.axis_index("dom")
+    core, z, x = lax.rem(me, 2), lax.rem(me // 2, N_Z), me // (2 * N_Z)
+    barrier = pltpu.get_barrier_semaphore()
+
+    get_map = pltpu.make_async_copy(map_hbm, map_ref, local_sem.at[0])
+    get_map.start()
+    get_feat = pltpu.make_async_copy(feat_hbm, feat_ref, local_sem.at[1])
+    get_feat.start()
+    x_rows = N_Z * HOT_DEV
+    half = N_X * x_rows
+    own_at = pl.ds(pl.multiple_of(core * half + (x * N_Z + z) * HOT_DEV, HOT_DEV), HOT_DEV)
+    keep_hub = pltpu.make_async_copy(feat_hbm.at[pl.ds(0, HOT_DEV)], table_ref.at[own_at], local_sem.at[2])
+    keep_hub.start()
+
+    def peer(step):
+        k = lax.rem(step, 8)
+        dz = lax.rem(N_Z + 4 + (lax.rem(k, 2) * 2 - 1) * ((k + 1) // 2), N_Z)
+        dxc = lax.rem(step // 8 + 1, 8)
+        other = (lax.rem(x + dxc // 2, N_X) * N_Z + lax.rem(z + dz, N_Z)) * 2 + lax.rem(core + lax.rem(dxc, 2), 2)
+        return other, {"dom": other}
+
+    def greet(step, carry):
+        pl.semaphore_signal(barrier, inc=1, device_id=peer(step)[1], device_id_type=MESH)
+        return carry
+
+    lax.fori_loop(0, parts - 1, greet, 0)
+
+    place_ids(hop2_ref, hop1_ref, seed_ref, ids_ref)
+    ids_down = pltpu.make_async_copy(ids_ref, ids_smem, local_sem.at[3])
+    ids_down.start()
+    get_feat.wait()
+
+    def widen(step, carry):
+        at = pl.ds(pl.multiple_of(step * 64, 64), 64)
+        wide[at, :] = feat_ref[at, :].astype(jnp.float32)
+        return carry
+
+    lax.fori_loop(0, node_rows // 64, widen, 0)
+    keep_hub.wait()
+    pl.semaphore_wait(barrier, parts - 1)
+
+    def hub_copy(at, level, where):
+        return pltpu.make_async_remote_copy(
+            table_ref.at[at], table_ref.at[at], hub_send.at[level], hub_recv.at[level],
+            device_id=where, device_id_type=MESH,
+        )
+
+    def hub_wait(rows, level):
+        return hub_copy(pl.ds(0, rows), level, peer(0)[1])
+
+    def send_z(step, carry):
+        hub_copy(own_at, 0, {"dom": (x * N_Z + lax.rem(z + step, N_Z)) * 2 + core}).start()
+        return carry
+
+    def x_at(step):
+        return pl.ds(pl.multiple_of(core * half + lax.rem(x + step, N_X) * x_rows, x_rows), x_rows)
+
+    def send_x(step, carry):
+        hub_copy(x_at(0), 1, {"dom": (lax.rem(x + step, N_X) * N_Z + z) * 2 + core}).start()
+        return carry
+
+    def send_core(step, carry):
+        hub_copy(x_at(step), 2, {"dom": me + 1 - 2 * core}).start()
+        return carry
+
+    lax.fori_loop(1, N_Z, send_z, 0)
+    get_map.wait()
+    ids_down.wait()
+
+    def lookup(step, carry):
+        lookup_step(step, ids_ref, ids_smem, map_ref, stage_a, stage_b, pos_ref)
+        return carry
+
+    groups = -(-ID_ROWS // 4)
+    lax.fori_loop(0, groups // 3, lookup, 0)
+    hub_wait((N_Z - 1) * HOT_DEV, 0).wait_recv()
+    lax.fori_loop(1, N_X, send_x, 0)
+    lax.fori_loop(0, 1, send_core, 0)
+    lax.fori_loop(groups // 3, groups, lookup, 0)
+    for r in range(groups * 4, pos_ref.shape[0]):
+        pos_ref[r : r + 1, :] = jnp.zeros((1, LANES), jnp.int32)
+    assign(
+        pos_ref, own_ref, val_ref, slot_ref, addr_ref, req_ref, parts=parts, shift=shift, cap_row=cap_row,
+    )
+    ask_at = pl.ds(0, 1)
+    keep_req = pltpu.make_async_copy(req_ref.at[me], inbox.at[me], local_sem.at[4])
+    keep_req.start()
+
+    def ask(step, carry):
+        other, where = peer(step)
+        pltpu.make_async_remote_copy(
+            req_ref.at[other, ask_at], inbox.at[me, ask_at], req_send, req_recv, device_id=where, device_id_type=MESH
+        ).start()
+        return carry
+
+    lax.fori_loop(0, parts - 1, ask, 0)
+    most = pl.ds(0, parts - 1)
+    asked = pltpu.make_async_remote_copy(
+        req_ref.at[most, ask_at], inbox.at[most, ask_at], req_send, req_recv,
+        device_id=peer(0)[1], device_id_type=MESH,
+    )
+    keep_req.wait()
+    asked.wait_recv()
+    to_scalar = pltpu.make_async_copy(inbox.at[:, ask_at], wanted, local_sem.at[5])
+    to_scalar.start()
+    to_scalar.wait()
+
+    def collect(other):
+        for i in range(cap_row):
+            row_stage[i : i + 1, :] = wide[pl.ds(wanted[other, 0, i], 1), :]
+        return row_stage[...].astype(jnp.bfloat16)
+
+    def rows_at(part):
+        return pl.ds(pl.multiple_of(HUB_ROWS + part * cap_row, 8), cap_row)
+
+    def serve(step, carry):
+        other, where = peer(step)
+        send[other] = collect(other)
+        pltpu.make_async_remote_copy(
+            send.at[other], table_ref.at[rows_at(me)], row_send, row_recv, device_id=where, device_id_type=MESH
+        ).start()
+        return carry
+
+    lax.fori_loop(0, parts - 1, serve, 0)
+    table_ref[rows_at(me), :] = collect(me)
+    hub_wait((N_X - 1) * x_rows, 1).wait_recv()
+    lax.fori_loop(1, N_X, send_core, 0)
+    asked.wait_send()
+    hub_wait((N_Z - 1) * HOT_DEV, 0).wait_send()
+    hub_wait((N_X - 1) * x_rows, 1).wait_send()
+    hub_wait(half, 2).wait()
+    pltpu.make_async_remote_copy(
+        send.at[most], send.at[most], row_send, row_recv, device_id=peer(0)[1], device_id_type=MESH
+    ).wait()
+
+
+def front(hop2, hop1, seed_ids, partition_map, features, cap_row):
+    parts = lax.axis_size("dom")
+    node_rows, feat = features.shape
+    vmem = pl.BlockSpec(memory_space=pltpu.VMEM)
+    hbm = pl.BlockSpec(memory_space=pl.ANY)
+    rows = round_up(ID_ROWS, 8)
     return pl.pallas_call(
-        kernel,
-        name="plan",
+        functools.partial(front_kernel, parts=parts, shift=node_rows.bit_length() - 1, cap_row=cap_row),
+        name="front",
         out_shape=(
-            jax.ShapeDtypeStruct((parts, round_up(cap_pad // LANES, 8), LANES), jnp.int32),
+            jax.ShapeDtypeStruct((HUB_ROWS + parts * cap_row, feat), features.dtype),
             jax.ShapeDtypeStruct((rows, LANES), jnp.int32),
         ),
-        in_specs=[pl.BlockSpec(memory_space=pltpu.VMEM)] * 2,
-        out_specs=(pl.BlockSpec(memory_space=pltpu.VMEM),) * 2,
-        scratch_shapes=[pltpu.VMEM((rows, LANES), jnp.int32)] * 4
-        + [pltpu.VMEM((3 * LANES, partition_map.size // LANES), jnp.bfloat16)],
-        compiler_params=pltpu.CompilerParams(vmem_limit_bytes=VMEM_LIMIT),
-        cost_estimate=pl.CostEstimate(flops=40_000_000, bytes_accessed=1_000_000, transcendentals=0),
-    )(ids, partition_map.reshape(-1, LANES))
+        in_specs=[vmem, vmem, vmem, hbm, hbm],
+        out_specs=(vmem, vmem),
+        scratch_shapes=[pltpu.VMEM((rows, LANES), jnp.int32)] * 5
+        + [
+            pltpu.VMEM((partition_map.size // LANES, LANES), jnp.int32),
+            pltpu.VMEM((node_rows, feat), features.dtype),
+            pltpu.VMEM((node_rows, feat), jnp.float32),
+            pltpu.VMEM((2 * LANES, LANES), jnp.int32),
+            pltpu.VMEM((2 * LANES, LANES), jnp.int32),
+            pltpu.VMEM((cap_row, feat), jnp.float32),
+            pltpu.VMEM((parts, 8, LANES), jnp.int32),
+            pltpu.VMEM((parts, 8, LANES), jnp.int32),
+            pltpu.VMEM((parts, cap_row, feat), features.dtype),
+            pltpu.SMEM((rows, LANES), jnp.int32),
+            pltpu.SMEM((parts, 1, LANES), jnp.int32),
+            pltpu.SemaphoreType.DMA((6,)),
+            pltpu.SemaphoreType.DMA,
+            pltpu.SemaphoreType.DMA,
+            pltpu.SemaphoreType.DMA((3,)),
+            pltpu.SemaphoreType.DMA((3,)),
+            pltpu.SemaphoreType.DMA,
+            pltpu.SemaphoreType.DMA,
+        ],
+        compiler_params=pltpu.CompilerParams(collective_id=2, has_side_effects=True, vmem_limit_bytes=VMEM_LIMIT),
+    )(hop2, hop1, seed_ids.reshape(1, -1), partition_map.reshape(-1, LANES), features)
 
 
 ROOT = 0.7978845608028654
@@ -171,15 +353,21 @@
 
     lax.fori_loop(0, table_ref.shape[0] // chunk, widen, 0)
 
+    half = fan_two // 2
+    top = half * fan_one
+
     def fetch(step, carry):
         j = step // (seeds // 8)
         block = step % (seeds // 8)
         base = pl.multiple_of(step * 8, 8)
+        seed = block * 8
+        own_row = jnp.where(j < 8, (top + j) * LANES, (top + j - 8) * LANES + seeds) + seed
         for k in range(8):
-            hop = (block * 8 + k) * fan_one + j
-            own_buf[pl.ds(base + k, 1), :] = wide[pl.ds(addr_ref[seeds + hop], 1), :]
-            first = seeds + hops + hop * fan_two
-            rows = [wide[pl.ds(addr_ref[first + m], 1), :] for m in range(fan_two)]
+            own_buf[pl.ds(base + k, 1), :] = wide[pl.ds(addr_ref[own_row + k], 1), :]
+            rows = [
+                wide[pl.ds(addr_ref[(m % half * fan_one + j) * LANES + m // half * seeds + seed + k], 1), :]
+                for m in range(fan_two)
+            ]
             far_buf[pl.ds(base + k, 1), :] = tree_sum(rows)
         return carry
 
@@ -187,8 +375,9 @@
 
     def fetch_seed(step, carry):
         base = pl.multiple_of(step * 8, 8)
+        first = (top + fan_one - 8) * LANES + seeds
         for k in range(8):
-            own_buf[pl.ds(hops + base + k, 1), :] = wide[pl.ds(addr_ref[base + k], 1), :]
+            own_buf[pl.ds(hops + base + k, 1), :] = wide[pl.ds(addr_ref[first + base + k], 1), :]
         return carry
 
     lax.fori_loop(0, seeds // 8, fetch_seed, 0)
@@ -275,154 +464,6 @@
     )
 
 
-def exchange_kernel(
-    req_ref, feat_ref, out_ref, inbox, wanted, wide, stage, send,
-    local_sem, req_send, req_recv, hub_send, hub_recv, row_send, row_recv, *, parts, asks,
-):
-    node_rows = feat_ref.shape[0]
-    cap_row = send.shape[1]
-    me = lax.axis_index("dom")
-    bits = parts.bit_length() - 1
-    barrier = pltpu.get_barrier_semaphore()
-
-    def partner(mask):
-        other = me ^ mask
-        return other, {"dom": other}
-
-    def greet(step, carry):
-        pl.semaphore_signal(barrier, inc=1, device_id=partner(step)[1], device_id_type=MESH)
-        return carry
-
-    lax.fori_loop(1, parts, greet, 0)
-    hub_at = pl.ds(0, HOT_DEV)
-    ask_at = pl.ds(0, asks)
-    keep_req = pltpu.make_async_copy(req_ref.at[me], inbox.at[me], local_sem.at[0])
-    keep_req.start()
-    keep_hub = pltpu.make_async_copy(feat_ref.at[hub_at], out_ref.at[me, hub_at], local_sem.at[1])
-    keep_hub.start()
-    pl.semaphore_wait(barrier, parts - 1)
-
-    def ask(step, carry):
-        other, at = partner(parts - step)
-        pltpu.make_async_remote_copy(
-            req_ref.at[other, ask_at], inbox.at[me, ask_at], req_send, req_recv, device_id=at, device_id_type=MESH
-        ).start()
-        return carry
-
-    lax.fori_loop(1, parts, ask, 0)
-    keep_hub.wait()
-
-    def held(level, index):
-        return me ^ (index * (parts >> level))
-
-    def share(level):
-        at = partner(parts >> (level + 1))[1]
-
-        def one(index, carry):
-            slot = held(level, index)
-            pltpu.make_async_remote_copy(
-                out_ref.at[slot, hub_at], out_ref.at[slot, hub_at], hub_send.at[level], hub_recv.at[level],
-                device_id=at, device_id_type=MESH,
-            ).start()
-            return carry
-
-        lax.fori_loop(0, 1 << level, one, 0)
-
-    def shared(level):
-        some = out_ref.at[pl.ds(0, 1 << level), hub_at]
-        return pltpu.make_async_remote_copy(
-            some, some, hub_send.at[level], hub_recv.at[level], device_id=partner(1)[1], device_id_type=MESH
-        )
-
-    share(0)
-
-    def widen(step, carry):
-        at = pl.ds(pl.multiple_of(step * 64, 64), 64)
-        wide[at, :] = feat_ref[at, :].astype(jnp.float32)
-        return carry
-
-    lax.fori_loop(0, node_rows // 64, widen, 0)
-    most = pl.ds(0, parts - 1)
-    asked = pltpu.make_async_remote_copy(
-        req_ref.at[most, ask_at], inbox.at[most, ask_at], req_send, req_recv,
-        device_id=partner(1)[1], device_id_type=MESH,
-    )
-    keep_req.wait()
-    asked.wait_recv()
-    to_scalar = pltpu.make_async_copy(inbox.at[:, ask_at], wanted, local_sem.at[2])
-    to_scalar.start()
-    to_scalar.wait()
-
-    def collect(other):
-        def block(step, carry):
-            base = pl.multiple_of(step * 16, 16)
-            row = step // (LANES // 16)
-            lane = lax.rem(step, LANES // 16) * 16
-            for k in range(16):
-                stage[pl.ds(base + k, 1), :] = wide[pl.ds(wanted[other, row, lane + k], 1), :]
-            return carry
-
-        lax.fori_loop(0, cap_row // 16, block, 0)
-        return stage[...].astype(jnp.bfloat16)
-
-    rows_at = pl.ds(HOT_DEV, cap_row)
-
-    def serve(step, carry):
-        other, at = partner(parts - step)
-        send[other] = collect(other)
-        pltpu.make_async_remote_copy(
-            send.at[other], out_ref.at[me, rows_at], row_send, row_recv, device_id=at, device_id_type=MESH
-        ).start()
-        return carry
-
-    served = 1
-    for level in range(1, bits):
-        until = max(1, parts * (level - 1) // bits)
-        lax.fori_loop(served, until, serve, 0)
-        served = until
-        shared(level - 1).wait_recv()
-        share(level)
-    lax.fori_loop(served, parts, serve, 0)
-    out_ref[me, HOT_DEV:, :] = collect(me)
-    rows = pltpu.make_async_remote_copy(
-        send.at[most], out_ref.at[most, rows_at], row_send, row_recv, device_id=partner(1)[1], device_id_type=MESH
-    )
-    asked.wait_send()
-    shared(bits - 1).wait_recv()
-    for level in range(bits):
-        shared(level).wait_send()
-    rows.wait()
-
-
-def exchange(request, features, cap_row, asks):
-    parts = lax.axis_size("dom")
-    bits = parts.bit_length() - 1
-    node_rows, feat = features.shape
-    vmem = pl.BlockSpec(memory_space=pltpu.VMEM)
-    return pl.pallas_call(
-        functools.partial(exchange_kernel, parts=parts, asks=asks),
-        name="exchange",
-        out_shape=jax.ShapeDtypeStruct((parts, HOT_DEV + cap_row, feat), features.dtype),
-        in_specs=[vmem, vmem],
-        out_specs=vmem,
-        scratch_shapes=[
-            pltpu.VMEM(request.shape, jnp.int32),
-            pltpu.SMEM((parts, asks, LANES), jnp.int32),
-            pltpu.VMEM((node_rows, feat), jnp.float32),
-            pltpu.VMEM((cap_row, feat), jnp.float32),
-            pltpu.VMEM((parts, cap_row, feat), features.dtype),
-            pltpu.SemaphoreType.DMA((3,)),
-            pltpu.SemaphoreType.DMA,
-            pltpu.SemaphoreType.DMA,
-            pltpu.SemaphoreType.DMA((bits,)),
-            pltpu.SemaphoreType.DMA((bits,)),
-            pltpu.SemaphoreType.DMA,
-            pltpu.SemaphoreType.DMA,
-        ],
-        compiler_params=pltpu.CompilerParams(collective_id=2, has_side_effects=True, vmem_limit_bytes=VMEM_LIMIT),
-    )(request, features)
-
-
 def pack_plan(feat, hidden, classes):
     halves = hidden // LANES
     one = 2 * feat * halves
@@ -614,19 +655,11 @@
     seeds = seed_ids.shape[0]
     fan_one = hop1_ids.shape[1]
     fan_two = hop2_ids.shape[2]
-    node_rows, feat = features.shape
+    feat = features.shape[1]
     tree_rows = 1 + fan_one + fan_one * fan_two
     cold_cap = tree_rows // 2 * (seeds // parts)
-    cap_row = round_up(cold_cap, 16)
-    cap_pad = round_up(cold_cap, LANES)
-    stride = HOT_DEV + cap_row
-    total = seeds * tree_rows
-    id_rows = total // LANES
-    spare = round_up(id_rows, 8) * LANES - total
-    wanted = [seed_ids, hop1_ids.reshape(-1), hop2_ids.reshape(-1), jnp.zeros((spare,), jnp.int32)]
-    ids = jnp.concatenate(wanted).reshape(-1, LANES)
-    request, addr = plan(ids, partition_map, parts, node_rows, stride, id_rows, cap_pad)
-    table = exchange(request, features, cap_row, cap_pad // LANES).reshape(parts * stride, feat)
+    cap_row = round_up(cold_cap, 8)
+    table, addr = front(hop2_ids.transpose(2, 1, 0), hop1_ids.T, seed_ids, partition_map, features, cap_row)
     hidden, classes = self_two.shape
     used = pack_plan(feat, hidden, classes)[-1]
     pack_rows = count * round_up(-(-used // count), 8)

time: 233 us -> 152 us (0.65)
  Pallas kernels: 228 us -> 151 us
  local copies, waits for them, and re-layouts: 3.74 us -> 0 us
    pallas_call x2 -> x1, Pallas kernels: 167 us -> 89.4 us  [front(): pl.pallas_call(functools.partial(front_kernel, parts=parts, shift=node_ro...]
where the time goes in v1:
time: 152 us
  Pallas kernels  151 us (99%)
    pallas_call x1, Pallas kernels, front(): pl.pallas_call(functools.partial(front_kernel, parts=parts, shift=node_ro...  89.4 us
    pallas_call x1, Pallas kernels, sum_everywhere(): pl.pallas_call(functools.partial(reduce_kernel, n_dom=n_dom, n_rep=n_rep,...  40.9 us
    pallas_call x1, Pallas kernels, model(): pl.pallas_call(functools.partial(model_kernel, seeds=seeds, fan_one=fan_o...  18.8 us

profile of v1, /device:TPU:1, one launch (start us, length us, event | category | flops | bytes accessed | tf_op | source)
XLA Modules:
  0.0 151.8 jit_solution(11818914558068573539)
XLA Ops:
  0.6 89.4 %front.1 = (bf16[22016,128]{1,0:T(8,128)(2,1)}, s32[88,128]{1,0:T(8,128)}) custom-call(s32[10,15,64]{2,1,0:T(8,128)} %bitcast.18, s32[15,64]{1,0:T(8,128)} %bitcast.20, s32[1,64]{1,0:T(1,128)} %bitcast.23, s32[4096,128]{1,0:T(8,128)} %bitcast.15, bf16[8192,128]{1,0:T(8,128)(2,1)} %feat_hbm.1), custom_call_target="tpu_custom_call" | custom-call | tf_op jit(solution)/shard_map/front/pallas_call | solution.py:285
  90.1 18.8 %model.1 = (f32[1,64]{1,0:T(1,128)}, f32[2048,128]{1,0:T(8,128)}) custom-call(s32[11264]{0:T(1024)} %bitcast.19, bf16[22016,128]{1,0:T(8,128)(2,1)} %get-tuple-element.18.table_ref, s32[1,64]{1,0:T(1,128)} %bitcast.24, bf16[128,256]{1,0:T(8,128)(2,1)} %self_one.1, bf16[128,256]{1,0:T(8,128)(2,1)} %neigh_one.1, f32[1,256]{1,0:T(1,128)} %bitcast.21, ...), custom_call_target="tpu_custom_call" | custom-call | flops 100000000 | bytes 4000000 | tf_op jit(solution)/shard_map/model/pallas_call | solution.py:435
  108.9 40.9 %sum_everywhere.1.pack_ref = f32[2048,128]{1,0:T(8,128)} custom-call(f32[2048,128]{1,0:T(8,128)} %get-tuple-element.20.part_ref), custom_call_target="tpu_custom_call" | custom-call | tf_op jit(solution)/shard_map/sum_everywhere/pallas_call | solution.py:631
  149.8 2.1 %unpack.1 = (f32[128,256]{1,0:T(8,128)}, f32[128,256]{1,0:T(8,128)}, f32[1,256]{1,0:T(1,128)}, f32[172,256]{1,0:T(8,128)}, f32[172,256]{1,0:T(8,128)}, /*index=5*/f32[1,172]{1,0:T(1,128)}) custom-call(f32[2048,128]{1,0:T(8,128)} %sum_everywhere.1.pack_ref), custom_call_target="tpu_custom_call" | custom-call | tf_op jit(solution)/shard_map/unpack/pallas_call | solution.py:511

commit v2 on v1

--- a/solution.py
+++ b/solution.py
@@ -10,7 +10,7 @@
 HOT_DEV = 256
 LANES = 128
 MESH = pl.DeviceIdType.MESH
-VMEM_LIMIT = 56 * 1024 * 1024
+MIB = 1024 * 1024
 
 
 def round_up(value, unit):
@@ -129,7 +129,59 @@
     for p in range(parts):
         req_ref[p, 0:1, :] = request[p : p + 1, :]
     hot_addr = (owner & 1) * (HUB_ROWS // 2) + (owner >> 1) * HOT_DEV + (local & (HOT_DEV - 1))
-    addr_ref[...] = jnp.where(is_cold, HUB_ROWS + owner * cap_row + slot_ref[...], hot_addr)
+    addr = jnp.where(is_cold, HUB_ROWS + owner * cap_row + slot_ref[...], hot_addr)
+    addr_ref[...] = jnp.clip(addr, 0, HUB_ROWS + parts * cap_row - 1)
+
+
+def tree_sum(values):
+    while len(values) > 1:
+        values = [a + b for a, b in zip(values[::2], values[1::2])] + (
+            [values[-1]] if len(values) % 2 else []
+        )
+    return values[0]
+
+
+def fetch_rows(addr_smem, wide, own_buf, far_buf, x_ref, *, seeds, fan_one, fan_two):
+    hops = seeds * fan_one
+    feat = wide.shape[1]
+    half = fan_two // 2
+    top = half * fan_one
+
+    def fetch(step, carry):
+        j = step // (seeds // 8)
+        seed = lax.rem(step, seeds // 8) * 8
+        base = pl.multiple_of(step * 8, 8)
+        late = j // 8
+        own_row = top + j - 8 * late
+        for k in range(8):
+            own_buf[pl.ds(base + k, 1), :] = wide[pl.ds(addr_smem[own_row, late * seeds + seed + k], 1), :]
+            rows = [
+                wide[pl.ds(addr_smem[m % half * fan_one + j, m // half * seeds + seed + k], 1), :]
+                for m in range(fan_two)
+            ]
+            far_buf[pl.ds(base + k, 1), :] = tree_sum(rows)
+        return carry
+
+    lax.fori_loop(0, hops // 8, fetch, 0)
+
+    def fetch_seed(step, carry):
+        base = pl.multiple_of(step * 8, 8)
+        for k in range(8):
+            own_buf[pl.ds(hops + base + k, 1), :] = wide[
+                pl.ds(addr_smem[top + fan_one - 8, seeds + base + k], 1), :
+            ]
+        return carry
+
+    lax.fori_loop(0, seeds // 8, fetch_seed, 0)
+    row_sum = jnp.zeros((seeds, feat), jnp.float32)
+    for j in range(fan_one):
+        at = slice(j * seeds, (j + 1) * seeds)
+        own = own_buf[at, :]
+        row_sum = row_sum + own
+        x_ref[at, :feat] = own.astype(jnp.bfloat16)
+        x_ref[at, feat:] = (far_buf[at, :] * (1.0 / fan_two)).astype(jnp.bfloat16)
+    x_ref[hops:, :feat] = own_buf[hops:, :].astype(jnp.bfloat16)
+    x_ref[hops:, feat:] = (row_sum * (1.0 / fan_one)).astype(jnp.bfloat16)
 
 
 def front_kernel(
@@ -179,7 +231,6 @@
 
     lax.fori_loop(0, node_rows // 64, widen, 0)
     keep_hub.wait()
-    pl.semaphore_wait(barrier, parts - 1)
 
     def hub_copy(at, level, where):
         return pltpu.make_async_remote_copy(
@@ -205,7 +256,6 @@
         hub_copy(x_at(step), 2, {"dom": me + 1 - 2 * core}).start()
         return carry
 
-    lax.fori_loop(1, N_Z, send_z, 0)
     get_map.wait()
     ids_down.wait()
 
@@ -215,10 +265,12 @@
 
     groups = -(-ID_ROWS // 4)
     lax.fori_loop(0, groups // 3, lookup, 0)
+    pl.semaphore_wait(barrier, parts - 1)
+    lax.fori_loop(1, N_Z, send_z, 0)
+    lax.fori_loop(groups // 3, groups, lookup, 0)
     hub_wait((N_Z - 1) * HOT_DEV, 0).wait_recv()
     lax.fori_loop(1, N_X, send_x, 0)
     lax.fori_loop(0, 1, send_core, 0)
-    lax.fori_loop(groups // 3, groups, lookup, 0)
     for r in range(groups * 4, pos_ref.shape[0]):
         pos_ref[r : r + 1, :] = jnp.zeros((1, LANES), jnp.int32)
     assign(
@@ -267,6 +319,7 @@
     table_ref[rows_at(me), :] = collect(me)
     hub_wait((N_X - 1) * x_rows, 1).wait_recv()
     lax.fori_loop(1, N_X, send_core, 0)
+
     asked.wait_send()
     hub_wait((N_Z - 1) * HOT_DEV, 0).wait_send()
     hub_wait((N_X - 1) * x_rows, 1).wait_send()
@@ -280,13 +333,14 @@
     parts = lax.axis_size("dom")
     node_rows, feat = features.shape
     vmem = pl.BlockSpec(memory_space=pltpu.VMEM)
-    hbm = pl.BlockSpec(memory_space=pl.ANY)
+    hbm = pl.BlockSpec(memory_space=pltpu.HBM)
     rows = round_up(ID_ROWS, 8)
+    table_rows = HUB_ROWS + parts * cap_row
     return pl.pallas_call(
         functools.partial(front_kernel, parts=parts, shift=node_rows.bit_length() - 1, cap_row=cap_row),
         name="front",
         out_shape=(
-            jax.ShapeDtypeStruct((HUB_ROWS + parts * cap_row, feat), features.dtype),
+            jax.ShapeDtypeStruct((table_rows, feat), features.dtype),
             jax.ShapeDtypeStruct((rows, LANES), jnp.int32),
         ),
         in_specs=[vmem, vmem, vmem, hbm, hbm],
@@ -312,8 +366,36 @@
             pltpu.SemaphoreType.DMA,
             pltpu.SemaphoreType.DMA,
         ],
-        compiler_params=pltpu.CompilerParams(collective_id=2, has_side_effects=True, vmem_limit_bytes=VMEM_LIMIT),
+        compiler_params=pltpu.CompilerParams(collective_id=2, has_side_effects=True, vmem_limit_bytes=24 * MIB),
     )(hop2, hop1, seed_ids.reshape(1, -1), partition_map.reshape(-1, LANES), features)
+
+def fetch_kernel(addr_smem, table_ref, x_ref, table_wide, own_buf, far_buf, *, seeds, fan_one, fan_two):
+    def widen(step, carry):
+        at = pl.ds(pl.multiple_of(step * 128, 128), 128)
+        table_wide[at, :] = table_ref[at, :].astype(jnp.float32)
+        return carry
+
+    lax.fori_loop(0, table_ref.shape[0] // 128, widen, 0)
+    fetch_rows(addr_smem, table_wide, own_buf, far_buf, x_ref, seeds=seeds, fan_one=fan_one, fan_two=fan_two)
+
+
+def fetch_all(addr, table, seeds, fan_one, fan_two):
+    feat = table.shape[1]
+    total = seeds * (1 + fan_one)
+    vmem = pl.BlockSpec(memory_space=pltpu.VMEM)
+    return pl.pallas_call(
+        functools.partial(fetch_kernel, seeds=seeds, fan_one=fan_one, fan_two=fan_two),
+        name="fetch",
+        out_shape=jax.ShapeDtypeStruct((total, 2 * feat), table.dtype),
+        in_specs=[pl.BlockSpec(memory_space=pltpu.SMEM), vmem],
+        out_specs=vmem,
+        scratch_shapes=[
+            pltpu.VMEM(table.shape, jnp.float32),
+            pltpu.VMEM((total, feat), jnp.float32),
+            pltpu.VMEM((total, feat), jnp.float32),
+        ],
+        compiler_params=pltpu.CompilerParams(vmem_limit_bytes=24 * MIB),
+    )(addr, table)
 
 
 ROOT = 0.7978845608028654
@@ -328,77 +410,90 @@
     return pre * half, slope
 
 
-def tree_sum(values):
-    while len(values) > 1:
-        values = [a + b for a, b in zip(values[::2], values[1::2])] + (
-            [values[-1]] if len(values) % 2 else []
-        )
-    return values[0]
-
-
-def model_kernel(
-    addr_ref, table_ref, label_ref, self_one, neigh_one, b_one_ref, self_two, neigh_two, b_two_ref,
-    loss_ref, pack_ref,
-    wide, x_buf, far_buf, own_buf, slope_buf, d_buf, *, seeds, fan_one, fan_two,
+N_REP = 4
+MEMBERS = N_X * N_REP * 2
+PART_TWO = 24
+PART_ONE = 16
+PART = PART_TWO + PART_ONE
+HIGH = 176
+
+
+def pack_two(part_ref, g_two, gb_two):
+    classes, width = g_two.shape
+    for h in range(width // LANES):
+        for b in range(HIGH // 8):
+            block = h * (HIGH // 8) + b
+            to = block % 3 * 8
+            rows = min(8, classes - b * 8)
+            part_ref[block // 3, to : to + rows, :] = g_two[
+                b * 8 : b * 8 + rows, h * LANES : (h + 1) * LANES
+            ].astype(jnp.bfloat16)
+            if rows < 8:
+                part_ref[block // 3, to + rows : to + 8, :] = jnp.zeros((8 - rows, LANES), jnp.bfloat16)
+    first = width // LANES * (HIGH // 8)
+    for block in range(first, MEMBERS * 3):
+        to = block % 3 * 8
+        part_ref[block // 3, to : to + 8, :] = jnp.zeros((8, LANES), jnp.bfloat16)
+    to = first % 3 * 8
+    part_ref[first // 3, to : to + 1, :] = gb_two[:, :LANES].astype(jnp.bfloat16)
+    part_ref[first // 3, to + 1 : to + 2, : classes - LANES] = gb_two[:, LANES:].astype(jnp.bfloat16)
+
+
+def pack_one(part_ref, g_one, gb_one):
+    halves = g_one.shape[1] // LANES
+    each = g_one.shape[0] // PART_ONE
+    for h in range(halves):
+        for i in range(each):
+            part_ref[h * each + i, PART_TWO:, :] = g_one[
+                i * PART_ONE : (i + 1) * PART_ONE, h * LANES : (h + 1) * LANES
+            ].astype(jnp.bfloat16)
+        part_ref[MEMBERS - 1, 16 + h : 17 + h, :] = gb_one[:, h * LANES : (h + 1) * LANES].astype(jnp.bfloat16)
+
+
+def dense_kernel(
+    x_ref, label_ref, self_one, neigh_one, b_one_ref, self_two, neigh_two, b_two_ref,
+    loss_ref, gathered,
+    slope_buf, d_buf, part_ref, box, z_box, send_sem, recv_sem, *, seeds, fan_one,
 ):
-    feat = table_ref.shape[1]
     hidden = self_one.shape[1]
     hops = seeds * fan_one
-    chunk = 64 if table_ref.shape[0] % 64 == 0 else 16
-
-    def widen(step, carry):
-        at = pl.ds(pl.multiple_of(step * chunk, chunk), chunk)
-        wide[at, :] = table_ref[at, :].astype(jnp.float32)
-        return carry
-
-    lax.fori_loop(0, table_ref.shape[0] // chunk, widen, 0)
-
-    half = fan_two // 2
-    top = half * fan_one
-
-    def fetch(step, carry):
-        j = step // (seeds // 8)
-        block = step % (seeds // 8)
-        base = pl.multiple_of(step * 8, 8)
-        seed = block * 8
-        own_row = jnp.where(j < 8, (top + j) * LANES, (top + j - 8) * LANES + seeds) + seed
-        for k in range(8):
-            own_buf[pl.ds(base + k, 1), :] = wide[pl.ds(addr_ref[own_row + k], 1), :]
-            rows = [
-                wide[pl.ds(addr_ref[(m % half * fan_one + j) * LANES + m // half * seeds + seed + k], 1), :]
-                for m in range(fan_two)
-            ]
-            far_buf[pl.ds(base + k, 1), :] = tree_sum(rows)
-        return carry
-
-    lax.fori_loop(0, hops // 8, fetch, 0)
-
-    def fetch_seed(step, carry):
-        base = pl.multiple_of(step * 8, 8)
-        first = (top + fan_one - 8) * LANES + seeds
-        for k in range(8):
-            own_buf[pl.ds(hops + base + k, 1), :] = wide[pl.ds(addr_ref[first + base + k], 1), :]
-        return carry
-
-    lax.fori_loop(0, seeds // 8, fetch_seed, 0)
+    me, y = lax.axis_index("dom"), lax.axis_index("rep")
+    core, z, x = lax.rem(me, 2), lax.rem(me // 2, N_Z), me // (2 * N_Z)
+    mine = (x * N_REP + y) * 2 + core
+    barrier = pltpu.get_barrier_semaphore()
+
+    def spread(k, size):
+        return lax.rem(size + size // 2 + (lax.rem(k, 2) * 2 - 1) * ((k + 1) // 2), size)
+
+    def near(step):
+        other_x = lax.rem(x + spread(step // 8, N_X), N_X)
+        other_y = lax.rem(y + spread(lax.rem(step // 2, N_REP), N_REP), N_REP)
+        other_core = lax.rem(core + lax.rem(step + 1, 2), 2)
+        where = {"dom": (other_x * N_Z + z) * 2 + other_core, "rep": other_y}
+        return (other_x * N_REP + other_y) * 2 + other_core, where
+
+    def far(step):
+        return {"dom": (x * N_Z + lax.rem(z + spread(step, N_Z), N_Z)) * 2 + core, "rep": y}
+
+    def greet_near(step, carry):
+        pl.semaphore_signal(barrier, inc=1, device_id=near(step)[1], device_id_type=MESH)
+        return carry
+
+    def greet_far(step, carry):
+        pl.semaphore_signal(barrier, inc=1, device_id=far(step), device_id_type=MESH)
+        return carry
+
+    lax.fori_loop(0, N_Z - 1, greet_far, 0)
+    lax.fori_loop(0, MEMBERS - 1, greet_near, 0)
 
     w_one = jnp.concatenate([self_one[...], neigh_one[...]], axis=0)
     w_two = jnp.concatenate([self_two[...], neigh_two[...]], axis=1)
     b_one = b_one_ref[...]
-    row_sum = jnp.zeros((seeds, feat), jnp.float32)
     hid_sum = jnp.zeros((seeds, hidden), jnp.float32)
-    for j in range(fan_one):
-        at = slice(j * seeds, (j + 1) * seeds)
-        own = own_buf[at, :]
-        row_sum = row_sum + own
-        x_buf[at, :feat] = own.astype(jnp.bfloat16)
-        x_buf[at, feat:] = (far_buf[at, :] * (1.0 / fan_two)).astype(jnp.bfloat16)
-    x_buf[hops:, :feat] = own_buf[hops:, :].astype(jnp.bfloat16)
-    x_buf[hops:, feat:] = (row_sum * (1.0 / fan_one)).astype(jnp.bfloat16)
     act = None
     for j in range(fan_one + 1):
         at = slice(j * seeds, (j + 1) * seeds)
-        act, slope = gelu_pair(dot_nn(x_buf[at, :], w_one) + b_one)
+        act, slope = gelu_pair(dot_nn(x_ref[at, :], w_one) + b_one)
         act = act.astype(jnp.bfloat16)
         slope_buf[at, :] = slope
         if j < fan_one:
@@ -414,8 +509,26 @@
     loss = jnp.sum(log_probs * target, axis=1, keepdims=True)
     loss_ref[...] = -jnp.sum(jnp.where(diagonal, loss, 0.0), axis=0, keepdims=True)
     d_logits = ((jnp.exp(log_probs) - target) * (1.0 / seeds)).astype(jnp.bfloat16)
-    g_two = dot_tn(d_logits, hid)
-    gb_two = jnp.sum(d_logits.astype(jnp.float32), axis=0, keepdims=True)
+    pack_two(part_ref, dot_tn(d_logits, hid), jnp.sum(d_logits.astype(jnp.float32), axis=0, keepdims=True))
+    pl.semaphore_wait(barrier, MEMBERS + N_Z - 2)
+
+    def copy(source, target, stage, where):
+        return pltpu.make_async_remote_copy(
+            source, target, send_sem.at[stage], recv_sem.at[stage], device_id=where, device_id_type=MESH
+        )
+
+    two_at, one_at = pl.ds(0, PART_TWO), pl.ds(PART_TWO, PART_ONE)
+
+    def send_two(step, carry):
+        other, where = near(step)
+
+        @pl.when(other < MEMBERS - 1)
+        def _():
+            copy(part_ref.at[other, two_at], box.at[mine, two_at], 0, where).start()
+
+        return carry
+
+    lax.fori_loop(0, MEMBERS - 1, send_two, 0)
     d_hid = dot_nn(d_logits, w_two)
     d_hop = d_hid[:, hidden:] * (1.0 / fan_one)
     for j in range(fan_one + 1):
@@ -423,37 +536,81 @@
         d_pre = ((d_hop if j < fan_one else d_hid[:, :hidden]) * slope_buf[at, :]).astype(jnp.bfloat16)
         d_buf[at, :] = d_pre
     gb_one = dot_nn(jnp.ones((8, d_buf.shape[0]), jnp.bfloat16), d_buf[...])[:1]
-    pack_gradients(pack_ref, dot_tn(x_buf[...], d_buf[...]), gb_one, g_two, gb_two)
-
-
-def model(addr, table, labels, self_one, neigh_one, bias_one, self_two, neigh_two, bias_two, fan_one, fan_two, pack_rows):
+    pack_one(part_ref, dot_tn(x_ref[...], d_buf[...]), gb_one)
+
+    def send_one(step, carry):
+        other, where = near(step)
+        copy(part_ref.at[other, one_at], box.at[mine, one_at], 0, where).start()
+
+        @pl.when(other == MEMBERS - 1)
+        def _():
+            copy(part_ref.at[other, two_at], box.at[mine, two_at], 0, where).start()
+
+        return carry
+
+    lax.fori_loop(0, MEMBERS - 1, send_one, 0)
+    box[mine] = part_ref[mine]
+    some = box.at[pl.ds(0, MEMBERS - 1)]
+    first = copy(some, some, 0, near(0)[1])
+    first.wait_recv()
+    total = box[0].astype(jnp.float32)
+    for i in range(1, MEMBERS):
+        total = total + box[i].astype(jnp.float32)
+    z_box[z] = total
+
+    def across(step, carry):
+        copy(z_box.at[z], z_box.at[z], 1, far(step)).start()
+        return carry
+
+    lax.fori_loop(0, N_Z - 1, across, 0)
+    some = z_box.at[pl.ds(0, N_Z - 1)]
+    second = copy(some, some, 1, far(0))
+    second.wait_recv()
+    total = z_box[0]
+    for i in range(1, N_Z):
+        total = total + z_box[i]
+    gathered[mine] = total.astype(jnp.bfloat16)
+
+    def back(step, carry):
+        copy(gathered.at[mine], gathered.at[mine], 2, near(step)[1]).start()
+        return carry
+
+    lax.fori_loop(0, MEMBERS - 1, back, 0)
+    some = gathered.at[pl.ds(0, MEMBERS - 1)]
+    third = copy(some, some, 2, near(0)[1])
+    third.wait_recv()
+    first.wait_send()
+    second.wait_send()
+    third.wait_send()
+
+
+def dense(x, labels, self_one, neigh_one, bias_one, self_two, neigh_two, bias_two, fan_one):
     seeds = labels.shape[0]
-    feat, hidden = self_one.shape
+    hidden = self_one.shape[1]
     classes = self_two.shape[1]
-    total = seeds * (1 + fan_one)
+    total = x.shape[0]
     vmem = pl.BlockSpec(memory_space=pltpu.VMEM)
     return pl.pallas_call(
-        functools.partial(model_kernel, seeds=seeds, fan_one=fan_one, fan_two=fan_two),
-        name="model",
+        functools.partial(dense_kernel, seeds=seeds, fan_one=fan_one),
+        name="dense",
         out_shape=(
             jax.ShapeDtypeStruct((1, seeds), jnp.float32),
-            jax.ShapeDtypeStruct((pack_rows, LANES), jnp.float32),
+            jax.ShapeDtypeStruct((MEMBERS, PART, LANES), jnp.bfloat16),
         ),
-        in_specs=[pl.BlockSpec(memory_space=pltpu.SMEM)] + [vmem] * 8,
+        in_specs=[vmem] * 8,
         out_specs=(vmem,) * 2,
         scratch_shapes=[
-            pltpu.VMEM(table.shape, jnp.float32),
-            pltpu.VMEM((total, 2 * feat), jnp.bfloat16),
-            pltpu.VMEM((total - seeds, feat), jnp.float32),
-            pltpu.VMEM((total, feat), jnp.float32),
             pltpu.VMEM((total, hidden), jnp.float32),
             pltpu.VMEM((total, hidden), jnp.bfloat16),
+            pltpu.VMEM((MEMBERS, PART, LANES), jnp.bfloat16),
+            pltpu.VMEM((MEMBERS, PART, LANES), jnp.bfloat16),
+            pltpu.VMEM((N_Z, PART, LANES), jnp.float32),
+            pltpu.SemaphoreType.DMA((3,)),
+            pltpu.SemaphoreType.DMA((3,)),
         ],
-        compiler_params=pltpu.CompilerParams(vmem_limit_bytes=VMEM_LIMIT),
-        cost_estimate=pl.CostEstimate(flops=100_000_000, bytes_accessed=4_000_000, transcendentals=0),
+        compiler_params=pltpu.CompilerParams(collective_id=1, has_side_effects=True, vmem_limit_bytes=16 * MIB),
     )(
-        addr,
-        table,
+        x,
         labels.reshape(1, seeds),
         self_one,
         neigh_one,
@@ -464,186 +621,43 @@
     )
 
 
-def pack_plan(feat, hidden, classes):
-    halves = hidden // LANES
-    one = 2 * feat * halves
-    high = round_up(classes, 8)
-    tail = one + 2 * halves * high
-    return halves, one, high, tail, tail + 8
-
-
-def pack_gradients(pack_ref, g_one, gb_one, g_two, gb_two):
-    hidden, feat = g_one.shape[1], g_one.shape[0] // 2
-    classes = g_two.shape[0]
-    halves, one, high, tail, used = pack_plan(feat, hidden, classes)
-    for h in range(halves):
-        pack_ref[h * 2 * feat : (h + 1) * 2 * feat, :] = g_one[:, h * LANES : (h + 1) * LANES]
-    pack_ref[one:, :] = jnp.zeros((pack_ref.shape[0] - one, LANES), jnp.float32)
-    for h in range(2 * halves):
-        pack_ref[one + h * high : one + h * high + classes, :] = g_two[:, h * LANES : (h + 1) * LANES]
-    for h in range(halves):
-        pack_ref[tail + h : tail + h + 1, :] = gb_one[:, h * LANES : (h + 1) * LANES]
-    pack_ref[tail + halves : tail + halves + 1, :] = gb_two[:, :LANES]
-    pack_ref[tail + halves + 1 : tail + halves + 2, : classes - LANES] = gb_two[:, LANES:]
-
-
-def unpack_kernel(pack_ref, self_one, neigh_one, bias_one, self_two, neigh_two, bias_two):
+def unpack_kernel(gathered, loss_in, loss_out, self_one, neigh_one, bias_one, self_two, neigh_two, bias_two):
     feat, hidden = self_one.shape
     classes = self_two.shape[0]
-    halves, one, high, tail, used = pack_plan(feat, hidden, classes)
+    loss_out[...] = loss_in[...]
+    halves = hidden // LANES
+    each = feat // PART_ONE
     for h in range(halves):
         cols = slice(h * LANES, (h + 1) * LANES)
-        at = h * 2 * feat
-        self_one[:, cols] = pack_ref[at : at + feat, :]
-        neigh_one[:, cols] = pack_ref[at + feat : at + 2 * feat, :]
-        at = one + h * high
-        self_two[:, cols] = pack_ref[at : at + classes, :]
-        at = one + (halves + h) * high
-        neigh_two[:, cols] = pack_ref[at : at + classes, :]
-        bias_one[:, cols] = pack_ref[tail + h : tail + h + 1, :]
-    bias_two[:, :LANES] = pack_ref[tail + halves : tail + halves + 1, :]
-    bias_two[:, LANES:] = pack_ref[tail + halves + 1 : tail + halves + 2, : classes - LANES]
-
-
-def unpack(packed, feat, hidden, classes):
+        for i in range(each):
+            at = slice(i * PART_ONE, (i + 1) * PART_ONE)
+            self_one[at, cols] = gathered[h * 2 * each + i, PART_TWO:, :].astype(jnp.float32)
+            neigh_one[at, cols] = gathered[h * 2 * each + each + i, PART_TWO:, :].astype(jnp.float32)
+        for b in range(HIGH // 8):
+            rows = min(8, classes - b * 8)
+            for k, out in enumerate((self_two, neigh_two)):
+                block = (k * halves + h) * (HIGH // 8) + b
+                to = block % 3 * 8
+                out[b * 8 : b * 8 + rows, cols] = gathered[block // 3, to : to + 8, :].astype(jnp.float32)[:rows]
+        bias_one[:, cols] = gathered[MEMBERS - 1, 16:24, :].astype(jnp.float32)[h : h + 1]
+    first = 2 * halves * (HIGH // 8)
+    to = first % 3 * 8
+    last = gathered[first // 3, to : to + 8, :].astype(jnp.float32)
+    bias_two[:, :LANES] = last[:1]
+    bias_two[:, LANES:] = last[1:2, : classes - LANES]
+
+
+def unpack(gathered, loss, feat, hidden, classes):
     vmem = pl.BlockSpec(memory_space=pltpu.VMEM)
-    shapes = [(feat, hidden), (feat, hidden), (1, hidden), (classes, hidden), (classes, hidden), (1, classes)]
+    shapes = [loss.shape, (feat, hidden), (feat, hidden), (1, hidden), (classes, hidden), (classes, hidden), (1, classes)]
     return pl.pallas_call(
         unpack_kernel,
         name="unpack",
         out_shape=tuple(jax.ShapeDtypeStruct(shape, jnp.float32) for shape in shapes),
-        in_specs=[vmem],
-        out_specs=(vmem,) * 6,
-        compiler_params=pltpu.CompilerParams(vmem_limit_bytes=VMEM_LIMIT),
-    )(packed)
-
-
-def reduce_kernel(
-    part_ref, out_ref, near_box, middle, far_box, gathered, send_sem, recv_sem, *, n_dom, n_rep, near,
-):
-    count = n_dom * n_rep
-    far = count // near
-    rows = part_ref.shape[0] // count
-    span = far * rows
-    me = lax.axis_index("dom") * n_rep + lax.axis_index("rep")
-    here, there = lax.rem(me, near), me // near
-    barrier = pltpu.get_barrier_semaphore()
-
-    def place(index):
-        return {"dom": index // n_rep, "rep": lax.rem(index, n_rep)}
-
-    def near_peer(step):
-        other = lax.rem(here + step, near)
-        return other, place(there * near + other)
-
-    def far_peer(step):
-        other = lax.rem(there + step, far)
-        return other, place(other * near + here)
-
-    def wide_at(index):
-        return pl.ds(pl.multiple_of(index * span, 8), span)
-
-    def thin_at(index):
-        return pl.ds(pl.multiple_of(index * rows, 8), rows)
-
-    def greet_near(step, carry):
-        pl.semaphore_signal(barrier, inc=1, device_id=near_peer(step)[1], device_id_type=MESH)
-        return carry
-
-    def greet_far(step, carry):
-        pl.semaphore_signal(barrier, inc=1, device_id=far_peer(step)[1], device_id_type=MESH)
-        return carry
-
-    lax.fori_loop(1, near, greet_near, 0)
-    lax.fori_loop(1, far, greet_far, 0)
-    pl.semaphore_wait(barrier, near + far - 2)
-
-    def copy(source, target, stage, where):
-        return pltpu.make_async_remote_copy(
-            source, target, send_sem.at[stage], recv_sem.at[stage], device_id=where, device_id_type=MESH
-        )
-
-    def out_near(step, carry):
-        other, where = near_peer(step)
-        copy(part_ref.at[wide_at(other)], near_box.at[wide_at(here)], 0, where).start()
-        return carry
-
-    lax.fori_loop(1, near, out_near, 0)
-    some = pl.ds(0, (near - 1) * span)
-    first = copy(part_ref.at[some], near_box.at[some], 0, near_peer(1)[1])
-    first.wait_recv()
-
-    def add_near(step, total):
-        return total + near_box[wide_at(near_peer(step)[0]), :]
-
-    middle[...] = lax.fori_loop(1, near, add_near, part_ref[wide_at(here), :])
-
-    def out_far(step, carry):
-        other, where = far_peer(step)
-        copy(middle.at[thin_at(other)], far_box.at[thin_at(there)], 1, where).start()
-        return carry
-
-    lax.fori_loop(1, far, out_far, 0)
-    some = pl.ds(0, (far - 1) * rows)
-    second = copy(middle.at[some], far_box.at[some], 1, far_peer(1)[1])
-    second.wait_recv()
-
-    def add_far(step, total):
-        return total + far_box[thin_at(far_peer(step)[0]), :]
-
-    total = lax.fori_loop(1, far, add_far, middle[thin_at(there), :])
-    mine = here * far + there
-    gathered[mine] = total.astype(gathered.dtype)
-
-    def back_far(step, carry):
-        copy(gathered.at[mine], gathered.at[mine], 2, far_peer(step)[1]).start()
-        return carry
-
-    lax.fori_loop(1, far, back_far, 0)
-    some = gathered.at[pl.ds(0, far - 1)]
-    third = copy(some, some, 2, far_peer(1)[1])
-    third.wait_recv()
-    group = gathered.at[pl.ds(here * far, far)]
-
-    def back_near(step, carry):
-        copy(group, group, 3, near_peer(step)[1]).start()
-        return carry
-
-    lax.fori_loop(1, near, back_near, 0)
-    some = gathered.at[pl.ds(0, (near - 1) * far)]
-    fourth = copy(some, some, 3, near_peer(1)[1])
-    fourth.wait_recv()
-    first.wait_send()
-    second.wait_send()
-    third.wait_send()
-    fourth.wait_send()
-    for index in range(count):
-        out_ref[index * rows : (index + 1) * rows, :] = gathered[index].astype(jnp.float32)
-
-
-def sum_everywhere(pieces):
-    n_dom, n_rep = lax.axis_size("dom"), lax.axis_size("rep")
-    count = n_dom * n_rep
-    near = 8
-    far = count // near
-    rows = pieces.shape[0] // count
-    vmem = pl.BlockSpec(memory_space=pltpu.VMEM)
-    return pl.pallas_call(
-        functools.partial(reduce_kernel, n_dom=n_dom, n_rep=n_rep, near=near),
-        name="sum_everywhere",
-        out_shape=jax.ShapeDtypeStruct(pieces.shape, jnp.float32),
-        in_specs=[vmem],
-        out_specs=vmem,
-        scratch_shapes=[
-            pltpu.VMEM(pieces.shape, jnp.float32),
-            pltpu.VMEM((far * rows, LANES), jnp.float32),
-            pltpu.VMEM((far * rows, LANES), jnp.float32),
-            pltpu.VMEM((count, rows, LANES), jnp.bfloat16),
-            pltpu.SemaphoreType.DMA((4,)),
-            pltpu.SemaphoreType.DMA((4,)),
-        ],
-        compiler_params=pltpu.CompilerParams(collective_id=1, has_side_effects=True, vmem_limit_bytes=VMEM_LIMIT),
-    )(pieces)
+        in_specs=[vmem] * 2,
+        out_specs=(vmem,) * 7,
+        compiler_params=pltpu.CompilerParams(vmem_limit_bytes=8 * MIB),
+    )(gathered, loss)
 
 
 def shards(
@@ -651,7 +665,6 @@
     self_one, neigh_one, bias_one, self_two, neigh_two, bias_two,
 ):
     parts = lax.axis_size("dom")
-    count = parts * lax.axis_size("rep")
     seeds = seed_ids.shape[0]
     fan_one = hop1_ids.shape[1]
     fan_two = hop2_ids.shape[2]
@@ -660,14 +673,10 @@
     cold_cap = tree_rows // 2 * (seeds // parts)
     cap_row = round_up(cold_cap, 8)
     table, addr = front(hop2_ids.transpose(2, 1, 0), hop1_ids.T, seed_ids, partition_map, features, cap_row)
+    x = fetch_all(addr, table, seeds, fan_one, fan_two)
     hidden, classes = self_two.shape
-    used = pack_plan(feat, hidden, classes)[-1]
-    pack_rows = count * round_up(-(-used // count), 8)
-    loss, pieces = model(
-        addr.reshape(-1), table, labels, self_one, neigh_one, bias_one, self_two, neigh_two, bias_two,
-        fan_one, fan_two, pack_rows,
-    )
-    grads = unpack(sum_everywhere(pieces), feat, hidden, classes)
+    loss, gathered = dense(x, labels, self_one, neigh_one, bias_one, self_two, neigh_two, bias_two, fan_one)
+    loss, *grads = unpack(gathered, loss, feat, hidden, classes)
     return (
         loss.reshape(-1), grads[0], grads[1], grads[2].reshape(-1),
         grads[3].T, grads[4].T, grads[5].reshape(-1),

time: 152 us -> 145 us (0.954)
  Pallas kernels: 151 us -> 138 us
  local copies, waits for them, and re-layouts: 0 us -> 5.46 us
    pallas_call x2, Pallas kernels: 59.7 us -> 47.2 us  [the longest x1 25.3 us: dense(): pl.pallas_call(functools.partial(dense_kernel, seeds=seeds, fan_one=fan_o...]
    unnamed x0 -> x24, local copies, waits for them, and re-layouts: none -> 5.46 us
where the time goes in v2:
time: 145 us
  Pallas kernels  138 us (95%)
  local copies, waits for them, and re-layouts  5.46 us (4%)
    pallas_call x1, Pallas kernels, front(): pl.pallas_call(functools.partial(front_kernel, parts=parts, shift=node_ro...  90.3 us
    pallas_call x1, Pallas kernels, dense(): pl.pallas_call(functools.partial(dense_kernel, seeds=seeds, fan_one=fan_o...  25.3 us
    pallas_call x1, Pallas kernels, fetch_all(): pl.pallas_call(functools.partial(fetch_kernel, seeds=seeds, fan_one=fan_o...  21.9 us
    unnamed x24, local copies, waits for them, and re-layouts  5.46 us

profile of v2, /device:TPU:1, one launch (start us, length us, event | category | flops | bytes accessed | tf_op | source)
XLA Modules:
  0.0 144.6 jit_solution(16114507580493451090)
XLA Ops:
  0.6 0.0 copy-start
  0.6 1.6 %copy-done = s32[524288]{0:T(1024)S(1)} copy-done((s32[524288]{0:T(1024)S(1)}, s32[524288]{0:T(1024)}, u32[]{:S(2)}) %copy-start) | copy-done | bytes 2097176
  2.2 0.0 copy-start.1
  2.2 1.6 %copy-done.1 = bf16[8192,128]{1,0:T(8,128)(2,1)S(1)} copy-done((bf16[8192,128]{1,0:T(8,128)(2,1)S(1)}, bf16[8192,128]{1,0:T(8,128)(2,1)}, u32[]{:S(2)}) %copy-start.1) | copy-done | bytes 2097176
  3.8 0.0 copy-start.4
  3.8 0.9 copy-done.4
  4.7 0.0 copy-start.7
  4.7 0.7 copy-done.7
  5.4 0.0 copy-start.10
  5.4 0.7 copy-done.10
  6.1 90.3 %front.1 = (bf16[22016,128]{1,0:T(8,128)(2,1)S(1)}, s32[88,128]{1,0:T(8,128)S(1)}) custom-call(s32[10,15,64]{2,1,0:T(8,128)S(1)} %bitcast.17, s32[15,64]{1,0:T(8,128)S(1)} %bitcast.18, s32[1,64]{1,0:T(1,128)S(1)} %bitcast.21, s32[4096,128]{1,0:T(8,128)S(1)} %bitcast.14, bf16[8192,128]{1,0:T(8,128)(2,1)S(1)} %copy-done.1), custom_call_target="tpu_custom_call" | custom-call | tf_op jit(solution)/shard_map/front/pallas_call | solution.py:339
  96.4 0.0 copy-start.2
  96.4 0.0 copy-start.3
  96.4 0.0 copy-start.5
  96.4 0.0 copy-start.6
  96.4 0.0 copy-start.8
  96.4 0.0 copy-start.9
  96.4 0.0 copy-start.11
  96.4 21.9 %fetch.1.x_ref = bf16[1024,256]{1,0:T(8,128)(2,1)S(1)} custom-call(s32[88,128]{1,0:T(8,128)S(1)} %get-tuple-element.18.addr_smem, bf16[22016,128]{1,0:T(8,128)(2,1)S(1)} %get-tuple-element.19.table_ref), custom_call_target="tpu_custom_call" | custom-call | tf_op jit(solution)/shard_map/fetch/pallas_call | solution.py:386
  118.4 0.0 copy-done.2
  118.4 0.0 copy-done.3
  118.4 0.0 copy-done.5
  118.4 0.0 copy-done.6
  118.4 0.0 copy-done.8
  118.4 0.0 copy-done.9
  118.5 0.0 copy-done.11
  118.5 25.3 %dense.1 = (f32[1,64]{1,0:T(1,128)S(1)}, bf16[32,40,128]{2,1,0:T(8,128)(2,1)S(1)}) custom-call(bf16[1024,256]{1,0:T(8,128)(2,1)S(1)} %fetch.1.x_ref, s32[1,64]{1,0:T(1,128)S(1)} %bitcast.22, bf16[128,256]{1,0:T(8,128)(2,1)S(1)} %copy-done.5, bf16[128,256]{1,0:T(8,128)(2,1)S(1)} %copy-done.6, f32[1,256]{1,0:T(1,128)S(1)} %bitcast.19, ...), custom_call_target="tpu_custom_call" | custom-call | tf_op jit(solution)/shard_map/dense/pallas_call | solution.py:593
  143.7 0.8 unpack.1
Async XLA Ops:
  0.6 1.6 %copy-start = (s32[524288]{0:T(1024)S(1)}, s32[524288]{0:T(1024)}, u32[]{:S(2)}) copy-start(s32[524288]{0:T(1024)} %param.13) | copy-start | bytes 6291460
  2.2 1.6 %copy-start.1 = (bf16[8192,128]{1,0:T(8,128)(2,1)S(1)}, bf16[8192,128]{1,0:T(8,128)(2,1)}, u32[]{:S(2)}) copy-start(bf16[8192,128]{1,0:T(8,128)(2,1)} %feat_hbm.1) | copy-start | bytes 6291460
  3.8 0.9 copy-start.4
  4.7 0.7 copy-start.7
  5.4 0.7 copy-start.10
  96.4 22.0 %copy-start.2 = (bf16[256,172]{0,1:T(8,128)(2,1)S(1)}, bf16[256,172]{0,1:T(8,128)(2,1)}, u32[]{:S(2)}) copy-start(bf16[256,172]{0,1:T(8,128)(2,1)} %param.21) | copy-start | bytes 264196
  96.4 22.0 %copy-start.3 = (bf16[256,172]{0,1:T(8,128)(2,1)S(1)}, bf16[256,172]{0,1:T(8,128)(2,1)}, u32[]{:S(2)}) copy-start(bf16[256,172]{0,1:T(8,128)(2,1)} %param.22) | copy-start | bytes 264196
  96.4 22.0 %copy-start.5 = (bf16[128,256]{1,0:T(8,128)(2,1)S(1)}, bf16[128,256]{1,0:T(8,128)(2,1)}, u32[]{:S(2)}) copy-start(bf16[128,256]{1,0:T(8,128)(2,1)} %self_one.1) | copy-start | bytes 196612
  96.4 22.0 %copy-start.6 = (bf16[128,256]{1,0:T(8,128)(2,1)S(1)}, bf16[128,256]{1,0:T(8,128)(2,1)}, u32[]{:S(2)}) copy-start(bf16[128,256]{1,0:T(8,128)(2,1)} %neigh_one.1) | copy-start | bytes 196612
  96.4 22.0 %copy-start.8 = (f32[256]{0:T(256)S(1)}, f32[256]{0:T(256)}, u32[]{:S(2)}) copy-start(f32[256]{0:T(256)} %param.20) | copy-start | bytes 3076
  96.4 22.0 %copy-start.9 = (f32[172]{0:T(256)S(1)}, f32[172]{0:T(256)}, u32[]{:S(2)}) copy-start(f32[172]{0:T(256)} %param.23) | copy-start | bytes 2068
  96.4 22.0 %copy-start.11 = (s32[64]{0:T(128)S(1)}, s32[64]{0:T(128)}, u32[]{:S(2)}) copy-start(s32[64]{0:T(128)} %param.17) | copy-start | bytes 772

commit v3 on v2

--- a/solution.py
+++ b/solution.py
@@ -50,8 +50,9 @@
 
 def gather_map(first, smem_ref, map_ref, stage):
     for r in range(stage.shape[0] // LANES):
+        high = smem_ref.at[first + r]
         for i in range(LANES):
-            stage[pl.ds(r * LANES + i, 1), :] = map_ref[pl.ds(smem_ref[first + r, i] >> 7, 1), :]
+            stage[r * LANES + i : r * LANES + i + 1, :] = map_ref[pl.ds(high[i], 1), :]
 
 
 def pick_lanes(first, ids_ref, stage, pos_ref):
@@ -147,22 +148,19 @@
     half = fan_two // 2
     top = half * fan_one
 
-    def fetch(step, carry):
-        j = step // (seeds // 8)
-        seed = lax.rem(step, seeds // 8) * 8
-        base = pl.multiple_of(step * 8, 8)
+    def fetch(j, carry):
         late = j // 8
-        own_row = top + j - 8 * late
-        for k in range(8):
-            own_buf[pl.ds(base + k, 1), :] = wide[pl.ds(addr_smem[own_row, late * seeds + seed + k], 1), :]
-            rows = [
-                wide[pl.ds(addr_smem[m % half * fan_one + j, m // half * seeds + seed + k], 1), :]
-                for m in range(fan_two)
-            ]
-            far_buf[pl.ds(base + k, 1), :] = tree_sum(rows)
-        return carry
-
-    lax.fori_loop(0, hops // 8, fetch, 0)
+        own_at = addr_smem.at[top + j - 8 * late, pl.ds(pl.multiple_of(late * seeds, seeds), seeds)]
+        far_at = [addr_smem.at[m * fan_one + j] for m in range(half)]
+        base = pl.multiple_of(j * seeds, seeds)
+        own_out, far_out = own_buf.at[pl.ds(base, seeds)], far_buf.at[pl.ds(base, seeds)]
+        for k in range(seeds):
+            own_out[k : k + 1, :] = wide[pl.ds(own_at[k], 1), :]
+            rows = [wide[pl.ds(far_at[m % half][m // half * seeds + k], 1), :] for m in range(fan_two)]
+            far_out[k : k + 1, :] = tree_sum(rows)
+        return carry
+
+    lax.fori_loop(0, fan_one, fetch, 0)
 
     def fetch_seed(step, carry):
         base = pl.multiple_of(step * 8, 8)
@@ -185,9 +183,9 @@
 
 
 def front_kernel(
-    hop2_ref, hop1_ref, seed_ref, map_hbm, feat_hbm,
+    hop2_hbm, hop1_hbm, seed_hbm, map_hbm, feat_hbm,
     table_ref, addr_ref,
-    ids_ref, pos_ref, own_ref, val_ref, slot_ref, map_ref, feat_ref, wide, stage_a, stage_b, row_stage,
+    hop2_ref, hop1_ref, seed_ref, ids_ref, pos_ref, own_ref, val_ref, slot_ref, map_ref, feat_ref, wide, stage_a, stage_b, row_stage,
     req_ref, inbox, send, ids_smem, wanted,
     local_sem, req_send, req_recv, hub_send, hub_recv, row_send, row_recv, *, parts, shift, cap_row,
 ):
@@ -196,6 +194,12 @@
     core, z, x = lax.rem(me, 2), lax.rem(me // 2, N_Z), me // (2 * N_Z)
     barrier = pltpu.get_barrier_semaphore()
 
+    get_ids = [
+        pltpu.make_async_copy(source, target, local_sem.at[6 + n])
+        for n, (source, target) in enumerate(((hop2_hbm, hop2_ref), (hop1_hbm, hop1_ref), (seed_hbm, seed_ref)))
+    ]
+    for each in get_ids:
+        each.start()
     get_map = pltpu.make_async_copy(map_hbm, map_ref, local_sem.at[0])
     get_map.start()
     get_feat = pltpu.make_async_copy(feat_hbm, feat_ref, local_sem.at[1])
@@ -219,8 +223,11 @@
 
     lax.fori_loop(0, parts - 1, greet, 0)
 
+    for each in get_ids:
+        each.wait()
     place_ids(hop2_ref, hop1_ref, seed_ref, ids_ref)
-    ids_down = pltpu.make_async_copy(ids_ref, ids_smem, local_sem.at[3])
+    slot_ref[...] = ids_ref[...] >> 7
+    ids_down = pltpu.make_async_copy(slot_ref, ids_smem, local_sem.at[3])
     ids_down.start()
     get_feat.wait()
 
@@ -248,9 +255,14 @@
     def x_at(step):
         return pl.ds(pl.multiple_of(core * half + lax.rem(x + step, N_X) * x_rows, x_rows), x_rows)
 
-    def send_x(step, carry):
-        hub_copy(x_at(0), 1, {"dom": (lax.rem(x + step, N_X) * N_Z + z) * 2 + core}).start()
-        return carry
+    def send_x(first, rows):
+        at = pl.ds(pl.multiple_of(core * half + x * x_rows + first, 8), rows)
+
+        def one(step, carry):
+            hub_copy(at, 1, {"dom": (lax.rem(x + step, N_X) * N_Z + z) * 2 + core}).start()
+            return carry
+
+        lax.fori_loop(1, N_X, one, 0)
 
     def send_core(step, carry):
         hub_copy(x_at(step), 2, {"dom": me + 1 - 2 * core}).start()
@@ -268,9 +280,6 @@
     pl.semaphore_wait(barrier, parts - 1)
     lax.fori_loop(1, N_Z, send_z, 0)
     lax.fori_loop(groups // 3, groups, lookup, 0)
-    hub_wait((N_Z - 1) * HOT_DEV, 0).wait_recv()
-    lax.fori_loop(1, N_X, send_x, 0)
-    lax.fori_loop(0, 1, send_core, 0)
     for r in range(groups * 4, pos_ref.shape[0]):
         pos_ref[r : r + 1, :] = jnp.zeros((1, LANES), jnp.int32)
     assign(
@@ -288,6 +297,11 @@
         return carry
 
     lax.fori_loop(0, parts - 1, ask, 0)
+    hub_wait((N_Z - 1) * HOT_DEV, 0).wait_recv()
+    x_early = x_rows // 4
+    x_each = (x_rows - x_early) // parts
+    send_x(0, x_early)
+    lax.fori_loop(0, 1, send_core, 0)
     most = pl.ds(0, parts - 1)
     asked = pltpu.make_async_remote_copy(
         req_ref.at[most, ask_at], inbox.at[most, ask_at], req_send, req_recv,
@@ -300,8 +314,9 @@
     to_scalar.wait()
 
     def collect(other):
+        asked_rows = wanted.at[other, 0]
         for i in range(cap_row):
-            row_stage[i : i + 1, :] = wide[pl.ds(wanted[other, 0, i], 1), :]
+            row_stage[i : i + 1, :] = wide[pl.ds(asked_rows[i], 1), :]
         return row_stage[...].astype(jnp.bfloat16)
 
     def rows_at(part):
@@ -313,9 +328,11 @@
         pltpu.make_async_remote_copy(
             send.at[other], table_ref.at[rows_at(me)], row_send, row_recv, device_id=where, device_id_type=MESH
         ).start()
+        send_x(x_early + step * x_each, x_each)
         return carry
 
     lax.fori_loop(0, parts - 1, serve, 0)
+    send_x(x_early + (parts - 1) * x_each, x_each)
     table_ref[rows_at(me), :] = collect(me)
     hub_wait((N_X - 1) * x_rows, 1).wait_recv()
     lax.fori_loop(1, N_X, send_core, 0)
@@ -343,9 +360,14 @@
             jax.ShapeDtypeStruct((table_rows, feat), features.dtype),
             jax.ShapeDtypeStruct((rows, LANES), jnp.int32),
         ),
-        in_specs=[vmem, vmem, vmem, hbm, hbm],
+        in_specs=[hbm] * 5,
         out_specs=(vmem, vmem),
-        scratch_shapes=[pltpu.VMEM((rows, LANES), jnp.int32)] * 5
+        scratch_shapes=[
+            pltpu.VMEM(hop2.shape, jnp.int32),
+            pltpu.VMEM(hop1.shape, jnp.int32),
+            pltpu.VMEM((1, seed_ids.size), jnp.int32),
+        ]
+        + [pltpu.VMEM((rows, LANES), jnp.int32)] * 5
         + [
             pltpu.VMEM((partition_map.size // LANES, LANES), jnp.int32),
             pltpu.VMEM((node_rows, feat), features.dtype),
@@ -358,7 +380,7 @@
             pltpu.VMEM((parts, cap_row, feat), features.dtype),
             pltpu.SMEM((rows, LANES), jnp.int32),
             pltpu.SMEM((parts, 1, LANES), jnp.int32),
-            pltpu.SemaphoreType.DMA((6,)),
+            pltpu.SemaphoreType.DMA((9,)),
             pltpu.SemaphoreType.DMA,
             pltpu.SemaphoreType.DMA,
             pltpu.SemaphoreType.DMA((3,)),
@@ -367,7 +389,12 @@
             pltpu.SemaphoreType.DMA,
         ],
         compiler_params=pltpu.CompilerParams(collective_id=2, has_side_effects=True, vmem_limit_bytes=24 * MIB),
-    )(hop2, hop1, seed_ids.reshape(1, -1), partition_map.reshape(-1, LANES), features)
+    )(
+        *(
+            pltpu.with_memory_space_constraint(each, pltpu.HBM)
+            for each in (hop2, hop1, seed_ids.reshape(1, -1), partition_map.reshape(-1, LANES), features)
+        )
+    )
 
 def fetch_kernel(addr_smem, table_ref, x_ref, table_wide, own_buf, far_buf, *, seeds, fan_one, fan_two):
     def widen(step, carry):

time: 145 us -> 111 us (0.77)
  Pallas kernels: 138 us -> 110 us
  local copies, waits for them, and re-layouts: 5.46 us -> 0.04 us
    pallas_call x1, Pallas kernels: 90.3 us -> 75.4 us  [front(): pl.pallas_call(functools.partial(front_kernel, parts=parts, shift=node_ro...]
    pallas_call x1, Pallas kernels: 21.9 us -> 9.31 us  [fetch_all(): pl.pallas_call(functools.partial(fetch_kernel, seeds=seeds, fan_one=fan_o...]
    unnamed x24 -> x14, local copies, waits for them, and re-layouts: 5.46 us -> 0.04 us
where the time goes in v3:
time: 111 us
  Pallas kernels  110 us (99%)
    pallas_call x1, Pallas kernels, front(): pl.pallas_call(functools.partial(front_kernel, parts=parts, shift=node_ro...  75.4 us
    pallas_call x1, Pallas kernels, dense(): pl.pallas_call(functools.partial(dense_kernel, seeds=seeds, fan_one=fan_o...  24.9 us
    pallas_call x1, Pallas kernels, fetch_all(): pl.pallas_call(functools.partial(fetch_kernel, seeds=seeds, fan_one=fan_o...  9.31 us

profile of v3, /device:TPU:1, one launch (start us, length us, event | category | flops | bytes accessed | tf_op | source)
XLA Modules:
  0.0 111.2 jit_solution(13571922553732282196)
XLA Ops:
  0.6 75.4 %front.1 = (bf16[22016,128]{1,0:T(8,128)(2,1)S(1)}, s32[88,128]{1,0:T(8,128)S(1)}) custom-call(s32[10,15,64]{2,1,0:T(8,128)} %bitcast.20, s32[15,64]{1,0:T(8,128)} %bitcast.21, s32[1,64]{1,0:T(1,128)} %bitcast.22, s32[4096,128]{1,0:T(8,128)} %bitcast.19, bf16[8192,128]{1,0:T(8,128)(2,1)} %feat_hbm.1), custom_call_target="tpu_custom_call" | custom-call | tf_op jit(solution)/shard_map/front/pallas_call | solution.py:356
  76.0 0.0 copy-start
  76.0 0.0 copy-start.1
  76.0 0.0 copy-start.2
  76.0 0.0 copy-start.3
  76.0 0.0 copy-start.4
  76.1 0.0 copy-start.5
  76.1 0.0 copy-start.6
  76.1 9.3 %fetch.1.x_ref = bf16[1024,256]{1,0:T(8,128)(2,1)S(1)} custom-call(s32[88,128]{1,0:T(8,128)S(1)} %get-tuple-element.18.addr_smem, bf16[22016,128]{1,0:T(8,128)(2,1)S(1)} %get-tuple-element.19.table_ref), custom_call_target="tpu_custom_call" | custom-call | tf_op jit(solution)/shard_map/fetch/pallas_call | solution.py:413
  85.4 0.0 copy-done
  85.4 0.0 copy-done.1
  85.4 0.0 copy-done.2
  85.4 0.0 copy-done.3
  85.4 0.0 copy-done.4
  85.4 0.0 copy-done.5
  85.5 0.0 copy-done.6
  85.5 24.9 %dense.1 = (f32[1,64]{1,0:T(1,128)S(1)}, bf16[32,40,128]{2,1,0:T(8,128)(2,1)S(1)}) custom-call(bf16[1024,256]{1,0:T(8,128)(2,1)S(1)} %fetch.1.x_ref, s32[1,64]{1,0:T(1,128)S(1)} %bitcast.18, bf16[128,256]{1,0:T(8,128)(2,1)S(1)} %copy-done.2, bf16[128,256]{1,0:T(8,128)(2,1)S(1)} %copy-done.3, f32[1,256]{1,0:T(1,128)S(1)} %bitcast.16, ...), custom_call_target="tpu_custom_call" | custom-call | tf_op jit(solution)/shard_map/dense/pallas_call | solution.py:620
  110.4 0.8 unpack.1
Async XLA Ops:
  76.0 9.4 %copy-start = (bf16[256,172]{0,1:T(8,128)(2,1)S(1)}, bf16[256,172]{0,1:T(8,128)(2,1)}, u32[]{:S(2)}) copy-start(bf16[256,172]{0,1:T(8,128)(2,1)} %param.21) | copy-start | bytes 264196
  76.0 9.4 %copy-start.1 = (bf16[256,172]{0,1:T(8,128)(2,1)S(1)}, bf16[256,172]{0,1:T(8,128)(2,1)}, u32[]{:S(2)}) copy-start(bf16[256,172]{0,1:T(8,128)(2,1)} %param.22) | copy-start | bytes 264196
  76.0 9.4 %copy-start.2 = (bf16[128,256]{1,0:T(8,128)(2,1)S(1)}, bf16[128,256]{1,0:T(8,128)(2,1)}, u32[]{:S(2)}) copy-start(bf16[128,256]{1,0:T(8,128)(2,1)} %self_one.1) | copy-start | bytes 196612
  76.0 9.4 %copy-start.3 = (bf16[128,256]{1,0:T(8,128)(2,1)S(1)}, bf16[128,256]{1,0:T(8,128)(2,1)}, u32[]{:S(2)}) copy-start(bf16[128,256]{1,0:T(8,128)(2,1)} %neigh_one.1) | copy-start | bytes 196612
  76.0 9.4 %copy-start.4 = (f32[256]{0:T(256)S(1)}, f32[256]{0:T(256)}, u32[]{:S(2)}) copy-start(f32[256]{0:T(256)} %param.20) | copy-start | bytes 3076
  76.1 9.4 %copy-start.5 = (f32[172]{0:T(256)S(1)}, f32[172]{0:T(256)}, u32[]{:S(2)}) copy-start(f32[172]{0:T(256)} %param.23) | copy-start | bytes 2068
  76.1 9.4 %copy-start.6 = (s32[64]{0:T(128)S(1)}, s32[64]{0:T(128)}, u32[]{:S(2)}) copy-start(s32[64]{0:T(128)} %param.17) | copy-start | bytes 772

commit v4 on v3

--- a/solution.py
+++ b/solution.py
@@ -187,11 +187,11 @@
     table_ref, addr_ref,
     hop2_ref, hop1_ref, seed_ref, ids_ref, pos_ref, own_ref, val_ref, slot_ref, map_ref, feat_ref, wide, stage_a, stage_b, row_stage,
     req_ref, inbox, send, ids_smem, wanted,
-    local_sem, req_send, req_recv, hub_send, hub_recv, row_send, row_recv, *, parts, shift, cap_row,
+    local_sem, scalar_sem, req_send, req_recv, hub_send, hub_recv, row_send, row_recv, *, parts, shift, cap_row,
 ):
     node_rows = feat_ref.shape[0]
     me = lax.axis_index("dom")
-    core, z, x = lax.rem(me, 2), lax.rem(me // 2, N_Z), me // (2 * N_Z)
+    core, z, x = me & 1, (me >> 1) & (N_Z - 1), me >> 4
     barrier = pltpu.get_barrier_semaphore()
 
     get_ids = [
@@ -210,18 +210,34 @@
     keep_hub = pltpu.make_async_copy(feat_hbm.at[pl.ds(0, HOT_DEV)], table_ref.at[own_at], local_sem.at[2])
     keep_hub.start()
 
-    def peer(step):
-        k = lax.rem(step, 8)
-        dz = lax.rem(N_Z + 4 + (lax.rem(k, 2) * 2 - 1) * ((k + 1) // 2), N_Z)
-        dxc = lax.rem(step // 8 + 1, 8)
-        other = (lax.rem(x + dxc // 2, N_X) * N_Z + lax.rem(z + dz, N_Z)) * 2 + lax.rem(core + lax.rem(dxc, 2), 2)
+    def turn_of(kind):
+        return ((kind >> 1) + 1) * (1 - 2 * (kind & 1))
+
+    def peer(dz, r, sign):
+        other = (((x + sign * (r >> 1)) & (N_X - 1)) << 4) + (((z + sign * dz) & (N_Z - 1)) << 1) + (core ^ (r & 1))
         return other, {"dom": other}
 
-    def greet(step, carry):
-        pl.semaphore_signal(barrier, inc=1, device_id=peer(step)[1], device_id_type=MESH)
-        return carry
-
-    lax.fori_loop(0, parts - 1, greet, 0)
+    def all_peers(act):
+        def kind(k, carry):
+            def one(r, inner):
+                act(k, k * 8 + r, *peer(turn_of(k), r, 1))
+                return inner
+
+            lax.fori_loop(0, 8, one, 0)
+            return carry
+
+        lax.fori_loop(0, N_Z - 1, kind, 0)
+
+        def flat(r, carry):
+            act(N_Z - 1, (N_Z - 1) * 8 + r - 1, *peer(0, r, 1))
+            return carry
+
+        lax.fori_loop(1, 8, flat, 0)
+
+    def greet(k, slot, other, where):
+        pl.semaphore_signal(barrier, inc=1, device_id=where, device_id_type=MESH)
+
+    all_peers(greet)
 
     for each in get_ids:
         each.wait()
@@ -246,23 +262,32 @@
         )
 
     def hub_wait(rows, level):
-        return hub_copy(pl.ds(0, rows), level, peer(0)[1])
+        return hub_copy(pl.ds(0, rows), level, peer(1, 0, 1)[1])
+
+    x_each = 72
+    x_early = x_rows - (parts - 1) // (N_X - 1) * x_each
 
     def send_z(step, carry):
-        hub_copy(own_at, 0, {"dom": (x * N_Z + lax.rem(z + step, N_Z)) * 2 + core}).start()
+        hub_copy(own_at, 0, peer(step, 0, 1)[1]).start()
         return carry
 
     def x_at(step):
-        return pl.ds(pl.multiple_of(core * half + lax.rem(x + step, N_X) * x_rows, x_rows), x_rows)
+        return pl.ds(pl.multiple_of(core * half + ((x + step) & (N_X - 1)) * x_rows, x_rows), x_rows)
 
     def send_x(first, rows):
         at = pl.ds(pl.multiple_of(core * half + x * x_rows + first, 8), rows)
 
         def one(step, carry):
-            hub_copy(at, 1, {"dom": (lax.rem(x + step, N_X) * N_Z + z) * 2 + core}).start()
+            hub_copy(at, 1, peer(0, 2 * step, 1)[1]).start()
             return carry
 
         lax.fori_loop(1, N_X, one, 0)
+
+    def send_x_one(step):
+        turn = step // (N_X - 1)
+        first = x_early + turn * x_each
+        at = pl.ds(pl.multiple_of(core * half + x * x_rows + first, 8), x_each)
+        hub_copy(at, 1, peer(0, 2 * (step - turn * (N_X - 1) + 1), 1)[1]).start()
 
     def send_core(step, carry):
         hub_copy(x_at(step), 2, {"dom": me + 1 - 2 * core}).start()
@@ -276,45 +301,48 @@
         return carry
 
     groups = -(-ID_ROWS // 4)
-    lax.fori_loop(0, groups // 3, lookup, 0)
+    lax.fori_loop(0, groups // 2, lookup, 0)
     pl.semaphore_wait(barrier, parts - 1)
     lax.fori_loop(1, N_Z, send_z, 0)
-    lax.fori_loop(groups // 3, groups, lookup, 0)
+    lax.fori_loop(groups // 2, groups, lookup, 0)
     for r in range(groups * 4, pos_ref.shape[0]):
         pos_ref[r : r + 1, :] = jnp.zeros((1, LANES), jnp.int32)
     assign(
         pos_ref, own_ref, val_ref, slot_ref, addr_ref, req_ref, parts=parts, shift=shift, cap_row=cap_row,
     )
     ask_at = pl.ds(0, 1)
-    keep_req = pltpu.make_async_copy(req_ref.at[me], inbox.at[me], local_sem.at[4])
+    keep_req = pltpu.make_async_copy(req_ref.at[me], inbox.at[parts - 1], local_sem.at[4])
     keep_req.start()
 
-    def ask(step, carry):
-        other, where = peer(step)
+    def ask(k, slot, other, where):
         pltpu.make_async_remote_copy(
-            req_ref.at[other, ask_at], inbox.at[me, ask_at], req_send, req_recv, device_id=where, device_id_type=MESH
+            req_ref.at[other, ask_at], inbox.at[slot, ask_at], req_send, req_recv.at[k],
+            device_id=where, device_id_type=MESH,
         ).start()
-        return carry
-
-    lax.fori_loop(0, parts - 1, ask, 0)
+
+    all_peers(ask)
     hub_wait((N_Z - 1) * HOT_DEV, 0).wait_recv()
-    x_early = x_rows // 4
-    x_each = (x_rows - x_early) // parts
     send_x(0, x_early)
     lax.fori_loop(0, 1, send_core, 0)
     most = pl.ds(0, parts - 1)
-    asked = pltpu.make_async_remote_copy(
-        req_ref.at[most, ask_at], inbox.at[most, ask_at], req_send, req_recv,
-        device_id=peer(0)[1], device_id_type=MESH,
-    )
+
+    def asked(k, count):
+        some = pl.ds(0, count)
+        return pltpu.make_async_remote_copy(
+            req_ref.at[some, ask_at], inbox.at[some, ask_at], req_send, req_recv.at[k],
+            device_id=peer(1, 0, 1)[1], device_id_type=MESH,
+        )
+
+    def to_scalar(k):
+        at = pl.ds(k * 8, 8)
+        return pltpu.make_async_copy(inbox.at[at, ask_at], wanted.at[at], scalar_sem.at[k])
+
+    asked(0, 8).wait_recv()
+    to_scalar(0).start()
     keep_req.wait()
-    asked.wait_recv()
-    to_scalar = pltpu.make_async_copy(inbox.at[:, ask_at], wanted, local_sem.at[5])
-    to_scalar.start()
-    to_scalar.wait()
-
-    def collect(other):
-        asked_rows = wanted.at[other, 0]
+
+    def collect(slot):
+        asked_rows = wanted.at[slot, 0]
         for i in range(cap_row):
             row_stage[i : i + 1, :] = wide[pl.ds(asked_rows[i], 1), :]
         return row_stage[...].astype(jnp.bfloat16)
@@ -322,27 +350,49 @@
     def rows_at(part):
         return pl.ds(pl.multiple_of(HUB_ROWS + part * cap_row, 8), cap_row)
 
-    def serve(step, carry):
-        other, where = peer(step)
-        send[other] = collect(other)
+    def serve(slot, dz, r):
+        where = peer(dz, r, -1)[1]
+        send[slot] = collect(slot)
         pltpu.make_async_remote_copy(
-            send.at[other], table_ref.at[rows_at(me)], row_send, row_recv, device_id=where, device_id_type=MESH
+            send.at[slot], table_ref.at[rows_at(me)], row_send, row_recv, device_id=where, device_id_type=MESH
         ).start()
-        send_x(x_early + step * x_each, x_each)
-        return carry
-
-    lax.fori_loop(0, parts - 1, serve, 0)
-    send_x(x_early + (parts - 1) * x_each, x_each)
-    table_ref[rows_at(me), :] = collect(me)
+        send_x_one(slot)
+
+    def serve_kind(k, carry):
+        to_scalar(k).wait()
+
+        @pl.when(k < N_Z - 2)
+        def _():
+            asked(k + 1, 8).wait_recv()
+            to_scalar(k + 1).start()
+
+        def one(r, inner):
+            serve(k * 8 + r, turn_of(k), r)
+            return inner
+
+        lax.fori_loop(0, 8, one, 0)
+        return carry
+
+    lax.fori_loop(0, N_Z - 1, serve_kind, 0)
+    asked(N_Z - 1, 7).wait_recv()
+    to_scalar(N_Z - 1).start()
+    to_scalar(N_Z - 1).wait()
+
+    def serve_flat(r, carry):
+        serve((N_Z - 1) * 8 + r - 1, 0, r)
+        return carry
+
+    lax.fori_loop(1, 8, serve_flat, 0)
+    table_ref[rows_at(me), :] = collect(parts - 1)
     hub_wait((N_X - 1) * x_rows, 1).wait_recv()
     lax.fori_loop(1, N_X, send_core, 0)
 
-    asked.wait_send()
+    asked(0, parts - 1).wait_send()
     hub_wait((N_Z - 1) * HOT_DEV, 0).wait_send()
     hub_wait((N_X - 1) * x_rows, 1).wait_send()
     hub_wait(half, 2).wait()
     pltpu.make_async_remote_copy(
-        send.at[most], send.at[most], row_send, row_recv, device_id=peer(0)[1], device_id_type=MESH
+        send.at[most], send.at[most], row_send, row_recv, device_id=peer(1, 0, 1)[1], device_id_type=MESH
     ).wait()
 
 
@@ -381,8 +431,9 @@
             pltpu.SMEM((rows, LANES), jnp.int32),
             pltpu.SMEM((parts, 1, LANES), jnp.int32),
             pltpu.SemaphoreType.DMA((9,)),
+            pltpu.SemaphoreType.DMA((N_Z,)),
             pltpu.SemaphoreType.DMA,
-            pltpu.SemaphoreType.DMA,
+            pltpu.SemaphoreType.DMA((N_Z,)),
             pltpu.SemaphoreType.DMA((3,)),
             pltpu.SemaphoreType.DMA((3,)),
             pltpu.SemaphoreType.DMA,
@@ -439,68 +490,77 @@
 
 N_REP = 4
 MEMBERS = N_X * N_REP * 2
-PART_TWO = 24
-PART_ONE = 16
+PART_TWO = 16
+PART_ONE = 24
 PART = PART_TWO + PART_ONE
 HIGH = 176
 
 
+def early_at(block):
+    return block // 2, block % 2 * 8
+
+
+def late_at(block):
+    return block // 3, PART_TWO + block % 3 * 8
+
+
+def two_at_block(block):
+    early = MEMBERS * 2
+    return early_at(block) if block < early else late_at(block - early)
+
+
+def put(part_ref, where, tile):
+    member, to = where
+    rows, lanes = tile.shape
+    part_ref[member, to : to + rows, :lanes] = tile.astype(jnp.bfloat16)
+
+
 def pack_two(part_ref, g_two, gb_two):
     classes, width = g_two.shape
+    blocks = width // LANES * (HIGH // 8)
+    for late in range(blocks - MEMBERS * 2, MEMBERS * 3):
+        put(part_ref, late_at(late), jnp.zeros((8, LANES), jnp.float32))
     for h in range(width // LANES):
+        cols = slice(h * LANES, (h + 1) * LANES)
         for b in range(HIGH // 8):
-            block = h * (HIGH // 8) + b
-            to = block % 3 * 8
-            rows = min(8, classes - b * 8)
-            part_ref[block // 3, to : to + rows, :] = g_two[
-                b * 8 : b * 8 + rows, h * LANES : (h + 1) * LANES
-            ].astype(jnp.bfloat16)
-            if rows < 8:
-                part_ref[block // 3, to + rows : to + 8, :] = jnp.zeros((8 - rows, LANES), jnp.bfloat16)
-    first = width // LANES * (HIGH // 8)
-    for block in range(first, MEMBERS * 3):
-        to = block % 3 * 8
-        part_ref[block // 3, to : to + 8, :] = jnp.zeros((8, LANES), jnp.bfloat16)
-    to = first % 3 * 8
-    part_ref[first // 3, to : to + 1, :] = gb_two[:, :LANES].astype(jnp.bfloat16)
-    part_ref[first // 3, to + 1 : to + 2, : classes - LANES] = gb_two[:, LANES:].astype(jnp.bfloat16)
-
-
-def pack_one(part_ref, g_one, gb_one):
+            tile = g_two[b * 8 : min(b * 8 + 8, classes), cols]
+            if tile.shape[0] < 8:
+                tile = jnp.concatenate([tile, jnp.zeros((8 - tile.shape[0], LANES), jnp.float32)], axis=0)
+            put(part_ref, two_at_block(h * (HIGH // 8) + b), tile)
+    member, to = two_at_block(blocks)
+    put(part_ref, (member, to), gb_two[:, :LANES])
+    put(part_ref, (member, to + 1), gb_two[:, LANES:])
+
+
+def pack_one(part_ref, g_one, gb_one, first):
     halves = g_one.shape[1] // LANES
-    each = g_one.shape[0] // PART_ONE
+    each = g_one.shape[0] // 8
+    member, to = two_at_block(first)
     for h in range(halves):
+        cols = slice(h * LANES, (h + 1) * LANES)
         for i in range(each):
-            part_ref[h * each + i, PART_TWO:, :] = g_one[
-                i * PART_ONE : (i + 1) * PART_ONE, h * LANES : (h + 1) * LANES
-            ].astype(jnp.bfloat16)
-        part_ref[MEMBERS - 1, 16 + h : 17 + h, :] = gb_one[:, h * LANES : (h + 1) * LANES].astype(jnp.bfloat16)
+            put(part_ref, two_at_block(first + 1 + h * each + i), g_one[i * 8 : i * 8 + 8, cols])
+        put(part_ref, (member, to + h), gb_one[:, cols])
 
 
 def dense_kernel(
     x_ref, label_ref, self_one, neigh_one, b_one_ref, self_two, neigh_two, b_two_ref,
     loss_ref, gathered,
-    slope_buf, d_buf, part_ref, box, z_box, send_sem, recv_sem, *, seeds, fan_one,
+    slope_buf, d_buf, part_ref, box, z_two, z_one, send_sem, recv_sem, *, seeds, fan_one,
 ):
     hidden = self_one.shape[1]
     hops = seeds * fan_one
     me, y = lax.axis_index("dom"), lax.axis_index("rep")
-    core, z, x = lax.rem(me, 2), lax.rem(me // 2, N_Z), me // (2 * N_Z)
+    core, z, x = me & 1, (me >> 1) & (N_Z - 1), me >> 4
     mine = (x * N_REP + y) * 2 + core
     barrier = pltpu.get_barrier_semaphore()
 
-    def spread(k, size):
-        return lax.rem(size + size // 2 + (lax.rem(k, 2) * 2 - 1) * ((k + 1) // 2), size)
-
     def near(step):
-        other_x = lax.rem(x + spread(step // 8, N_X), N_X)
-        other_y = lax.rem(y + spread(lax.rem(step // 2, N_REP), N_REP), N_REP)
-        other_core = lax.rem(core + lax.rem(step + 1, 2), 2)
-        where = {"dom": (other_x * N_Z + z) * 2 + other_core, "rep": other_y}
-        return (other_x * N_REP + other_y) * 2 + other_core, where
+        other = mine ^ (MEMBERS - 1 - step)
+        return other, {"dom": ((other >> 3) << 4) + (z << 1) + (other & 1), "rep": (other >> 1) & (N_REP - 1)}
 
     def far(step):
-        return {"dom": (x * N_Z + lax.rem(z + spread(step, N_Z), N_Z)) * 2 + core, "rep": y}
+        return {"dom": (x << 4) + (((z + 4 + ((step + 1) >> 1) * (1 - 2 * (step & 1))) & (N_Z - 1)) << 1) + core, "rep": y}
 
     def greet_near(step, carry):
         pl.semaphore_signal(barrier, inc=1, device_id=near(step)[1], device_id_type=MESH)
@@ -548,11 +608,7 @@
 
     def send_two(step, carry):
         other, where = near(step)
-
-        @pl.when(other < MEMBERS - 1)
-        def _():
-            copy(part_ref.at[other, two_at], box.at[mine, two_at], 0, where).start()
-
+        copy(part_ref.at[other, two_at], box.at[mine, two_at], 0, where).start()
         return carry
 
     lax.fori_loop(0, MEMBERS - 1, send_two, 0)
@@ -563,52 +619,68 @@
         d_pre = ((d_hop if j < fan_one else d_hid[:, :hidden]) * slope_buf[at, :]).astype(jnp.bfloat16)
         d_buf[at, :] = d_pre
     gb_one = dot_nn(jnp.ones((8, d_buf.shape[0]), jnp.bfloat16), d_buf[...])[:1]
-    pack_one(part_ref, dot_tn(x_ref[...], d_buf[...]), gb_one)
+    pack_one(part_ref, dot_tn(x_ref[...], d_buf[...]), gb_one, 2 * hidden // LANES * (HIGH // 8) + 1)
 
     def send_one(step, carry):
         other, where = near(step)
-        copy(part_ref.at[other, one_at], box.at[mine, one_at], 0, where).start()
-
-        @pl.when(other == MEMBERS - 1)
-        def _():
-            copy(part_ref.at[other, two_at], box.at[mine, two_at], 0, where).start()
-
+        copy(part_ref.at[other, one_at], box.at[mine, one_at], 1, where).start()
         return carry
 
     lax.fori_loop(0, MEMBERS - 1, send_one, 0)
     box[mine] = part_ref[mine]
-    some = box.at[pl.ds(0, MEMBERS - 1)]
-    first = copy(some, some, 0, near(0)[1])
-    first.wait_recv()
-    total = box[0].astype(jnp.float32)
-    for i in range(1, MEMBERS):
-        total = total + box[i].astype(jnp.float32)
-    z_box[z] = total
-
-    def across(step, carry):
-        copy(z_box.at[z], z_box.at[z], 1, far(step)).start()
-        return carry
-
-    lax.fori_loop(0, N_Z - 1, across, 0)
-    some = z_box.at[pl.ds(0, N_Z - 1)]
-    second = copy(some, some, 1, far(0))
-    second.wait_recv()
-    total = z_box[0]
-    for i in range(1, N_Z):
-        total = total + z_box[i]
-    gathered[mine] = total.astype(jnp.bfloat16)
-
-    def back(step, carry):
-        copy(gathered.at[mine], gathered.at[mine], 2, near(step)[1]).start()
-        return carry
-
-    lax.fori_loop(0, MEMBERS - 1, back, 0)
-    some = gathered.at[pl.ds(0, MEMBERS - 1)]
-    third = copy(some, some, 2, near(0)[1])
-    third.wait_recv()
-    first.wait_send()
-    second.wait_send()
-    third.wait_send()
+
+    def across(z_box, stage):
+        def one(step, carry):
+            copy(z_box.at[z], z_box.at[z], stage, far(step)).start()
+            return carry
+
+        lax.fori_loop(0, N_Z - 1, one, 0)
+
+    def back(at, stage):
+        def one(step, carry):
+            copy(gathered.at[mine, at], gathered.at[mine, at], stage, near(step)[1]).start()
+            return carry
+
+        lax.fori_loop(0, MEMBERS - 1, one, 0)
+
+    def of_near(ref, at, stage):
+        some = ref.at[pl.ds(0, MEMBERS - 1), at]
+        return copy(some, some, stage, near(0)[1])
+
+    def of_far(z_box, stage):
+        some = z_box.at[pl.ds(0, N_Z - 1)]
+        return copy(some, some, stage, far(0))
+
+    def total_near(first, rows):
+        total = box[0, first : first + rows, :].astype(jnp.float32)
+        for i in range(1, MEMBERS):
+            total = total + box[i, first : first + rows, :].astype(jnp.float32)
+        return total
+
+    def total_far(z_box):
+        total = z_box[0]
+        for i in range(1, N_Z):
+            total = total + z_box[i]
+        return total.astype(jnp.bfloat16)
+
+    of_near(box, two_at, 0).wait_recv()
+    z_two[z] = total_near(0, PART_TWO)
+    across(z_two, 2)
+    of_near(box, one_at, 1).wait_recv()
+    z_one[z] = total_near(PART_TWO, PART_ONE)
+    across(z_one, 3)
+    of_far(z_two, 2).wait_recv()
+    gathered[mine, :PART_TWO, :] = total_far(z_two)
+    back(two_at, 4)
+    of_far(z_one, 3).wait_recv()
+    gathered[mine, PART_TWO:, :] = total_far(z_one)
+    back(one_at, 5)
+    of_near(gathered, two_at, 4).wait()
+    of_near(gathered, one_at, 5).wait()
+    of_near(box, two_at, 0).wait_send()
+    of_near(box, one_at, 1).wait_send()
+    of_far(z_two, 2).wait_send()
+    of_far(z_one, 3).wait_send()
 
 
 def dense(x, labels, self_one, neigh_one, bias_one, self_two, neigh_two, bias_two, fan_one):
@@ -631,9 +703,10 @@
             pltpu.VMEM((total, hidden), jnp.bfloat16),
             pltpu.VMEM((MEMBERS, PART, LANES), jnp.bfloat16),
             pltpu.VMEM((MEMBERS, PART, LANES), jnp.bfloat16),
-            pltpu.VMEM((N_Z, PART, LANES), jnp.float32),
-            pltpu.SemaphoreType.DMA((3,)),
-            pltpu.SemaphoreType.DMA((3,)),
+            pltpu.VMEM((N_Z, PART_TWO, LANES), jnp.float32),
+            pltpu.VMEM((N_Z, PART_ONE, LANES), jnp.float32),
+            pltpu.SemaphoreType.DMA((6,)),
+            pltpu.SemaphoreType.DMA((6,)),
         ],
         compiler_params=pltpu.CompilerParams(collective_id=1, has_side_effects=True, vmem_limit_bytes=16 * MIB),
     )(
@@ -653,23 +726,25 @@
     classes = self_two.shape[0]
     loss_out[...] = loss_in[...]
     halves = hidden // LANES
-    each = feat // PART_ONE
+    each = feat // 8
+    blocks = 2 * halves * (HIGH // 8)
+
+    def tile_of(block):
+        member, to = two_at_block(block)
+        return gathered[member, to : to + 8, :].astype(jnp.float32)
+
     for h in range(halves):
         cols = slice(h * LANES, (h + 1) * LANES)
         for i in range(each):
-            at = slice(i * PART_ONE, (i + 1) * PART_ONE)
-            self_one[at, cols] = gathered[h * 2 * each + i, PART_TWO:, :].astype(jnp.float32)
-            neigh_one[at, cols] = gathered[h * 2 * each + each + i, PART_TWO:, :].astype(jnp.float32)
+            at = slice(i * 8, (i + 1) * 8)
+            self_one[at, cols] = tile_of(blocks + 2 + h * 2 * each + i)
+            neigh_one[at, cols] = tile_of(blocks + 2 + h * 2 * each + each + i)
         for b in range(HIGH // 8):
             rows = min(8, classes - b * 8)
             for k, out in enumerate((self_two, neigh_two)):
-                block = (k * halves + h) * (HIGH // 8) + b
-                to = block % 3 * 8
-                out[b * 8 : b * 8 + rows, cols] = gathered[block // 3, to : to + 8, :].astype(jnp.float32)[:rows]
-        bias_one[:, cols] = gathered[MEMBERS - 1, 16:24, :].astype(jnp.float32)[h : h + 1]
-    first = 2 * halves * (HIGH // 8)
-    to = first % 3 * 8
-    last = gathered[first // 3, to : to + 8, :].astype(jnp.float32)
+                out[b * 8 : b * 8 + rows, cols] = tile_of((k * halves + h) * (HIGH // 8) + b)[:rows]
+        bias_one[:, cols] = tile_of(blocks + 1)[h : h + 1]
+    last = tile_of(blocks)
     bias_two[:, :LANES] = last[:1]
     bias_two[:, LANES:] = last[1:2, : classes - LANES]
 

time: 111 us -> 108 us (0.973)
  Pallas kernels: 110 us -> 107 us
    pallas_call x1, Pallas kernels: 24.9 us -> 21.8 us  [dense(): pl.pallas_call(functools.partial(dense_kernel, seeds=seeds, fan_one=fan_o...]
where the time goes in v4:
time: 108 us; the launch traced here: 107 us
  Pallas kernels  107 us (99%)
    pallas_call x1, Pallas kernels, front(): pl.pallas_call(functools.partial(front_kernel, parts=parts, shift=node_ro...  74.7 us
    pallas_call x1, Pallas kernels, dense(): pl.pallas_call(functools.partial(dense_kernel, seeds=seeds, fan_one=fan_o...  21.8 us
    pallas_call x1, Pallas kernels, fetch_all(): pl.pallas_call(functools.partial(fetch_kernel, seeds=seeds, fan_one=fan_o...  9.31 us

profile of v4, /device:TPU:1, one launch (start us, length us, event | category | flops | bytes accessed | tf_op | source)
XLA Modules:
  0.0 107.4 jit_solution(7367948481616588960)
XLA Ops:
  0.6 74.7 %front.1 = (bf16[22016,128]{1,0:T(8,128)(2,1)S(1)}, s32[88,128]{1,0:T(8,128)S(1)}) custom-call(s32[10,15,64]{2,1,0:T(8,128)} %bitcast.20, s32[15,64]{1,0:T(8,128)} %bitcast.21, s32[1,64]{1,0:T(1,128)} %bitcast.22, s32[4096,128]{1,0:T(8,128)} %bitcast.19, bf16[8192,128]{1,0:T(8,128)(2,1)} %feat_hbm.1), custom_call_target="tpu_custom_call" | custom-call | tf_op jit(solution)/shard_map/front/pallas_call | solution.py:406
  75.3 0.0 copy-start
  75.3 0.0 copy-start.1
  75.3 0.0 copy-start.2
  75.3 0.0 copy-start.3
  75.3 0.0 copy-start.4
  75.4 0.0 copy-start.5
  75.4 0.0 copy-start.6
  75.4 9.3 %fetch.1.x_ref = bf16[1024,256]{1,0:T(8,128)(2,1)S(1)} custom-call(s32[88,128]{1,0:T(8,128)S(1)} %get-tuple-element.18.addr_smem, bf16[22016,128]{1,0:T(8,128)(2,1)S(1)} %get-tuple-element.19.table_ref), custom_call_target="tpu_custom_call" | custom-call | tf_op jit(solution)/shard_map/fetch/pallas_call | solution.py:464
  84.7 0.0 copy-done
  84.7 0.0 copy-done.1
  84.7 0.0 copy-done.2
  84.7 0.0 copy-done.3
  84.7 0.0 copy-done.4
  84.7 0.0 copy-done.5
  84.8 0.0 copy-done.6
  84.8 21.8 %dense.1 = (f32[1,64]{1,0:T(1,128)S(1)}, bf16[32,40,128]{2,1,0:T(8,128)(2,1)S(1)}) custom-call(bf16[1024,256]{1,0:T(8,128)(2,1)S(1)} %fetch.1.x_ref, s32[1,64]{1,0:T(1,128)S(1)} %bitcast.18, bf16[128,256]{1,0:T(8,128)(2,1)S(1)} %copy-done.2, bf16[128,256]{1,0:T(8,128)(2,1)S(1)} %copy-done.3, f32[1,256]{1,0:T(1,128)S(1)} %bitcast.16, ...), custom_call_target="tpu_custom_call" | custom-call | tf_op jit(solution)/shard_map/dense/pallas_call | solution.py:692
  106.6 0.8 unpack.1
Async XLA Ops:
  75.3 9.4 %copy-start = (bf16[256,172]{0,1:T(8,128)(2,1)S(1)}, bf16[256,172]{0,1:T(8,128)(2,1)}, u32[]{:S(2)}) copy-start(bf16[256,172]{0,1:T(8,128)(2,1)} %param.21) | copy-start | bytes 264196
  75.3 9.4 %copy-start.1 = (bf16[256,172]{0,1:T(8,128)(2,1)S(1)}, bf16[256,172]{0,1:T(8,128)(2,1)}, u32[]{:S(2)}) copy-start(bf16[256,172]{0,1:T(8,128)(2,1)} %param.22) | copy-start | bytes 264196
  75.3 9.4 %copy-start.2 = (bf16[128,256]{1,0:T(8,128)(2,1)S(1)}, bf16[128,256]{1,0:T(8,128)(2,1)}, u32[]{:S(2)}) copy-start(bf16[128,256]{1,0:T(8,128)(2,1)} %self_one.1) | copy-start | bytes 196612
  75.3 9.4 %copy-start.3 = (bf16[128,256]{1,0:T(8,128)(2,1)S(1)}, bf16[128,256]{1,0:T(8,128)(2,1)}, u32[]{:S(2)}) copy-start(bf16[128,256]{1,0:T(8,128)(2,1)} %neigh_one.1) | copy-start | bytes 196612
  75.3 9.4 %copy-start.4 = (f32[256]{0:T(256)S(1)}, f32[256]{0:T(256)}, u32[]{:S(2)}) copy-start(f32[256]{0:T(256)} %param.20) | copy-start | bytes 3076
  75.4 9.4 %copy-start.5 = (f32[172]{0:T(256)S(1)}, f32[172]{0:T(256)}, u32[]{:S(2)}) copy-start(f32[172]{0:T(256)} %param.23) | copy-start | bytes 2068
  75.4 9.4 %copy-start.6 = (s32[64]{0:T(128)S(1)}, s32[64]{0:T(128)}, u32[]{:S(2)}) copy-start(s32[64]{0:T(128)} %param.17) | copy-start | bytes 772
